TPU v7x, 32 devices: a whole 2x2x4 slice. The times are simulated.
32 devices in a mesh: space: 16 (over z, y, core), tensor: 2 (over x).
Axes of the slice: x: 2, y: 2, z: 4, core: 2. Of those that a mesh axis runs over, the one named last changes fastest.
Arguments:
- tokens: bfloat16 [14336, 1024], P('space', 'tensor'), may hold values from -6 to 6
- first_weight: bfloat16 [1024, 1024], P(None, 'tensor'), may hold values from -0.1875 to 0.1875
- second_weight: bfloat16 [1024, 1024], P(None, 'tensor'), may hold values from -0.1875 to 0.1875
- head_weight: bfloat16 [352, 1024], P('tensor'), may hold values from -0.1875 to 0.1875
- targets: float32 [352, 14336], P('tensor', 'space'), may hold values from -6 to 6
- land_mask: int32 [4, 14336], P(None, 'space'), may hold values from 0 to 1, as said below
- variable_kind: int32 [88], P('tensor'), may hold values from 0 to 2
- loss_scale: float32 [], replicated, may hold values from 630784 to 5046272
Outputs:
- loss: float32 [], replicated
- token_grad: float32 [14336, 1024], P('space', 'tensor')
- first_grad: float32 [1024, 1024], P('space', 'tensor')
- second_grad: float32 [1024, 1024], P('space', 'tensor')
- head_grad: float32 [352, 1024], P('tensor', 'space')
Inputs may be any that keep to these rules, and one draw needn't show every extreme that they name: `land_mask`: every aligned group of 8 entries along the last dimension holds at least one 1 and one 0. `variable_kind`: 0 scores a variable on all cells, 1 on land cells, 2 on ocean cells.
All inputs are finite; a program needn't handle non-finite values.
Results may differ from a plain program's by a relative error of at most 0.0056.
Values may be sent and summed in bfloat16 or wider, within the bound.
A program may use at most 64 MiB of HBM per device.

v0:
```python
import functools
import math

import jax
import jax.numpy as jnp
from jax import lax
from jax.experimental import pallas as pl
from jax.experimental.pallas import tpu as pltpu
from jax.sharding import PartitionSpec as P

PP = 4
PROW_DEV = 4
LONP = 224
MESH = pl.DeviceIdType.MESH
VMEM = pl.BlockSpec(memory_space=pltpu.VMEM)
ANY = pl.BlockSpec(memory_space=pl.ANY)


def bent(z):
    return (0.5 * z * (1.0 + lax.erf(z / math.sqrt(2.0)))).astype(jnp.bfloat16)


def slope(z):
    cdf = 0.5 * (1.0 + lax.erf(z / math.sqrt(2.0)))
    return cdf + z * jnp.exp(-0.5 * z * z) / math.sqrt(2.0 * math.pi)


def flipped(s, bit):
    step = 1 << bit
    return s + step - 2 * step * ((s // step) % 2)


def greet(partners):
    barrier = pltpu.get_barrier_semaphore()
    for partner in partners:
        pl.semaphore_signal(barrier, inc=1, device_id=partner, device_id_type=MESH)
    pl.semaphore_wait(barrier, len(partners))


def params(number, mib):
    return pltpu.CompilerParams(
        collective_id=number, has_side_effects=True, vmem_limit_bytes=mib * 2**20
    )


def gather_kernel(
    tok, one, two, head, tar, o_tok, o_one, o_two, o_head, o_tar, h_one, h_two, h_head, h_tok, h_tar, send, recv, local
):
    s, x = lax.axis_index("space"), lax.axis_index("tensor")
    other = 1 - x
    across, core, along, up = (s, other), (flipped(s, 0), x), (flipped(s, 1), x), (flipped(s, 2), x)
    mine = s % 8
    width = one.shape[1]
    rows = one.shape[0] // 8
    cols = head.shape[1] // 8
    half = o_tok.shape[0]

    def span(index, size):
        return pl.ds(pl.multiple_of(index * size, size), size)

    sources = [
        one.at[span(mine, rows), :],
        two.at[span(mine, rows), :],
        head.at[:, span(mine, cols)],
    ]
    places = [
        lambda side, q: o_one.at[span(q, rows), span(side, width)],
        lambda side, q: o_two.at[span(q, rows), span(side, width)],
        lambda side, q: o_head.at[side, :, span(q, cols)],
    ]

    greet([across, core, along, up])
    started = []

    def remote(src, dst, slot, target):
        copy = pltpu.make_async_remote_copy(
            src_ref=src,
            dst_ref=dst,
            send_sem=send.at[slot],
            recv_sem=recv.at[slot],
            device_id=target,
            device_id_type=MESH,
        )
        copy.start()
        started.append(copy)
        return copy

    firsts = [remote(sources[k], places[k](x, mine), 8 * k, across) for k in range(3)]
    extra = [
        remote(tok.at[span(other, half), :], o_tok.at[:, span(x, width)], 24, across),
        remote(tar.at[other], o_tar.at[x], 25, across),
    ]
    moves = [
        (one, h_one, o_one.at[:, span(x, width)]),
        (two, h_two, o_two.at[:, span(x, width)]),
        (head, h_head, o_head.at[x]),
        (tok.at[span(x, half), :], h_tok, o_tok.at[:, span(x, width)]),
        (tar.at[x], h_tar, o_tar.at[x]),
    ]
    held = [pltpu.make_async_copy(a, b, local.at[n]) for n, (a, b, _) in enumerate(moves)]
    own = [pltpu.make_async_copy(b, c, local.at[5 + n]) for n, (_, b, c) in enumerate(moves)]
    for copy in held:
        copy.start()
    for first, second in zip(held, own):
        first.wait()
        second.start()

    def pass_on(k, q, slot, target):
        piece = places[k](other, q)
        return remote(piece, piece, 8 * k + slot, target)

    ups, alongs, beyonds, ends = {}, {}, {}, []

    def stage_one(k):
        firsts[k].wait_recv()
        ups[k] = pass_on(k, mine, 1, up)
        alongs[k] = pass_on(k, mine, 2, along)
        ends.append(pass_on(k, mine, 4, core))

    def stage_two(k):
        ups[k].wait_recv()
        beyonds[k] = pass_on(k, flipped(mine, 2), 3, along)
        ends.append(pass_on(k, flipped(mine, 2), 5, core))

    def stage_three(k):
        alongs[k].wait_recv()
        ends.append(pass_on(k, flipped(mine, 1), 6, core))
        beyonds[k].wait_recv()
        ends.append(pass_on(k, flipped(flipped(mine, 1), 2), 7, core))

    stage_one(0)
    stage_one(1)
    stage_two(0)
    stage_one(2)
    stage_two(1)
    stage_two(2)
    for k in range(3):
        stage_three(k)
    for copy in ends + extra:
        copy.wait_recv()
    for copy in started:
        copy.wait_send()
    for copy in own:
        copy.wait()


def gather(tokens, first, second, head, targets):
    count, width = tokens.shape
    half = count // 2
    shape = jax.ShapeDtypeStruct
    return pl.pallas_call(
        gather_kernel,
        out_shape=(
            shape((half, 2 * width), tokens.dtype),
            shape((first.shape[0], 2 * first.shape[1]), first.dtype),
            shape((second.shape[0], 2 * second.shape[1]), second.dtype),
            shape((2,) + head.shape, head.dtype),
            shape(targets.shape, targets.dtype),
        ),
        in_specs=[ANY] * 5,
        out_specs=[ANY] * 5,
        scratch_shapes=[
            pltpu.VMEM(first.shape, first.dtype),
            pltpu.VMEM(second.shape, second.dtype),
            pltpu.VMEM(head.shape, head.dtype),
            pltpu.VMEM((half, width), tokens.dtype),
            pltpu.VMEM(targets.shape[1:], targets.dtype),
            pltpu.SemaphoreType.DMA((26,)),
            pltpu.SemaphoreType.DMA((26,)),
            pltpu.SemaphoreType.DMA((10,)),
        ],
        compiler_params=params(0, 16),
        name="gather",
    )(tokens, first, second, head, targets)


def total_kernel(groups, v_ref, o_ref, near, far, mid, send, recv):
    s, x = lax.axis_index("space"), lax.axis_index("tensor")
    low, high = s % 4, s // 4
    mine = x * 4 + low

    def near_peer(d):
        j = (mine + d) % 8
        return (high * 4 + j % 4, j // 4)

    def far_peer(d):
        return (((high + d) % groups) * 4 + low, x)

    greet([near_peer(d) for d in range(1, 8)] + [far_peer(d) for d in range(1, groups)])

    def share(src, slots, me, peers, base):
        copies = []
        for n, peer in enumerate(peers):
            copy = pltpu.make_async_remote_copy(
                src_ref=src,
                dst_ref=slots.at[me],
                send_sem=send.at[base + n],
                recv_sem=recv.at[base + n],
                device_id=peer,
                device_id_type=MESH,
            )
            copy.start()
            copies.append(copy)
        slots[me] = src[...]
        for copy in copies:
            copy.wait()

    share(v_ref, near, mine, [near_peer(d) for d in range(1, 8)], 0)
    mid[...] = jnp.sum(near[...], axis=0)
    share(mid, far, high, [far_peer(d) for d in range(1, groups)], 7)
    o_ref[...] = jnp.sum(far[...], axis=0)


def total(values):
    groups = lax.axis_size("space") // 4
    return pl.pallas_call(
        functools.partial(total_kernel, groups),
        out_shape=jax.ShapeDtypeStruct(values.shape, values.dtype),
        in_specs=[VMEM],
        out_specs=VMEM,
        scratch_shapes=[
            pltpu.VMEM((8,) + values.shape, values.dtype),
            pltpu.VMEM((groups,) + values.shape, values.dtype),
            pltpu.VMEM(values.shape, values.dtype),
            pltpu.SemaphoreType.DMA((6 + groups,)),
            pltpu.SemaphoreType.DMA((6 + groups,)),
        ],
        compiler_params=params(1, 4),
        name="total",
    )(values)


X = -1


def orders(bits):
    rest = list(range(3, bits))
    return ([0, 1, 2, X] + rest, [0, 2, 1, X] + rest, [0, X, 1, 2] + rest)


def pieces(bits, order, shape):
    found = []
    left = list(range(bits))[::-1]
    rows, cols = shape
    for bit in order:
        if bit == X:
            cols //= 2
        else:
            left.remove(bit)
        found.append((2,) * len(left) + (rows, cols))
    return found


def scatter_kernel(bits, plan, *refs):
    grads, tok, refs = refs[:3], refs[3], refs[4:]
    outs, o_tok, refs = refs[:3], refs[3], refs[4:]
    count = bits + 1
    parts = len(plan)
    landing = [refs[count * k : count * (k + 1)] for k in range(parts)]
    refs = refs[parts * count :]
    away = [refs[bits * k : bits * (k + 1)] for k in range(parts)]
    refs = refs[parts * bits :]
    kept = [refs[bits * k : bits * (k + 1)] for k in range(parts)]
    refs = refs[parts * bits :]
    near_in = refs[:parts]
    send, recv, local = refs[parts:]
    s, x = lax.axis_index("space"), lax.axis_index("tensor")

    def peer(bit):
        return (s, 1 - x) if bit == X else (flipped(s, bit), x)

    def part(ref, left, bit, near):
        if bit == X:
            width = ref.shape[-1] // 2
            side = x if near else 1 - x
            place = pl.ds(pl.multiple_of(side * width, width), width)
            return (slice(None),) * (len(ref.shape) - 1) + (place,)
        value = (s // (1 << bit)) % 2
        value = value if near else 1 - value
        return (slice(None),) * left.index(bit) + (value,)

    greet([peer(b) for b in [X] + list(range(bits))])
    copies = []

    def start(k, n, src):
        copy = pltpu.make_async_remote_copy(
            src_ref=src,
            dst_ref=landing[k][n],
            send_sem=send.at[k * count + n],
            recv_sem=recv.at[k * count + n],
            device_id=peer(plan[k][3][n]),
            device_id_type=MESH,
        )
        copy.start()
        copies.append(copy)
        return copy

    state = []
    for k, (which, first, rows, order) in enumerate(plan):
        left = list(range(bits))[::-1]
        ref = grads[which].at[(slice(None),) * bits + (pl.ds(first, rows),)]
        copy = start(k, 0, ref.at[part(ref, left, order[0], False)])
        left_now = [b for b in left if b != order[0]]
        state.append((ref.at[part(ref, left, order[0], True)], left_now, copy))
    inner = []
    for k in range(parts):
        ref, left, copy = state[k]
        inner.append(pltpu.make_async_copy(ref, near_in[k], local.at[k]))
        inner[k].start()
        state[k] = (near_in[k], left, copy)
    width = tok.shape[1] // 2
    tail = pltpu.make_async_remote_copy(
        src_ref=tok.at[:, pl.ds(pl.multiple_of((1 - x) * width, width), width)],
        dst_ref=o_tok,
        send_sem=send.at[parts * count],
        recv_sem=recv.at[parts * count],
        device_id=peer(X),
        device_id_type=MESH,
    )
    tail.start()
    copies.append(tail)

    def added(ref, arrived, index):
        return ref[index].astype(jnp.float32) + arrived[index].astype(jnp.float32)

    for n in range(count):
        for k, (which, first, rows, order) in enumerate(plan):
            ref, left, copy = state[k]
            arrived = landing[k][n]
            copy.wait_recv()
            if n == 0:
                inner[k].wait()
            if n == count - 1:
                outs[which][pl.ds(first, rows), :] = added(ref, arrived, ...)
                continue
            bit = order[n + 1]
            far = away[k][n]
            far[...] = added(ref, arrived, part(arrived, left, bit, False)).astype(far.dtype)
            copy = start(k, n + 1, far)
            near = kept[k][n]
            near[...] = added(ref, arrived, part(arrived, left, bit, True))
            state[k] = (near, [b for b in left if b != bit], copy)
    tail.wait_recv()
    for copy in copies:
        copy.wait_send()


def scatter(g_one, g_two, g_head, tok):
    size = lax.axis_size("space")
    bits = size.bit_length() - 1
    steps = orders(bits)
    grads = [g.reshape((2,) * bits + (g.shape[0] // size, g.shape[1])) for g in (g_one, g_two, g_head)]
    rows = grads[0].shape[-2]
    half = rows // 2
    plan = [
        (0, 0, half, steps[0]),
        (1, 0, half, steps[1]),
        (2, 0, rows, steps[2]),
        (0, half, half, steps[0]),
        (1, half, half, steps[1]),
    ]
    shapes = [pieces(bits, order, (n, grads[which].shape[-1])) for which, _, n, order in plan]
    scratch = [pltpu.VMEM(shape, jnp.bfloat16) for found in shapes for shape in found]
    scratch += [pltpu.VMEM(shape, jnp.bfloat16) for found in shapes for shape in found[1:]]
    scratch += [pltpu.VMEM(shape, jnp.float32) for found in shapes for shape in found[1:]]
    scratch += [pltpu.VMEM(found[0], jnp.bfloat16) for found in shapes]
    slots = len(plan) * (bits + 1) + 1
    outs = [shapes[which][-1][-1] for which in range(3)]
    return pl.pallas_call(
        functools.partial(scatter_kernel, bits, plan),
        out_shape=tuple(jax.ShapeDtypeStruct((rows, width), jnp.float32) for width in outs)
        + (jax.ShapeDtypeStruct((tok.shape[0], tok.shape[1] // 2), tok.dtype),),
        in_specs=[ANY] * 4,
        out_specs=[VMEM] * 3 + [ANY],
        scratch_shapes=scratch
        + [pltpu.SemaphoreType.DMA((n,)) for n in (slots, slots, len(plan))],
        compiler_params=params(2, 28),
        name="scatter",
    )(*grads, tok)


def mix(a, b, dims):
    return lax.dot_general(a, b, ((dims[:1], dims[1:]), ((), ())), preferred_element_type=jnp.float32)


def per_device(
    tokens, first_weight, second_weight, head_weight, targets, land_mask, variable_kind, loss_scale
):
    low = jnp.bfloat16
    count, width = tokens.shape
    half = count // 2
    rows = head_weight.shape[0]
    kinds = 2 * rows // PP
    s, x = lax.axis_index("space"), lax.axis_index("tensor")
    lanes = -(-(half + 1) // 128) * 128
    sent = jnp.stack([targets[:, :half], targets[:, half:]]).astype(low)
    label = jnp.repeat(variable_kind, PP).astype(low)[None, :, None]
    label = jnp.broadcast_to(label, (2, rows, lanes - half))
    sent = jnp.concatenate([sent, label], axis=2)
    toks, w_one, w_two, w_head, seen = gather(
        tokens, first_weight, second_weight, head_weight, sent
    )
    w_head = w_head.reshape(2 * rows, -1)
    goal = seen[:, :, :half].reshape(kinds, PP, half)
    kind = seen[:, :, half].reshape(kinds, PP)[:, :, None]

    position = s * count + x * half + jnp.arange(half, dtype=jnp.int32)
    cell = jnp.arange(PP, dtype=jnp.int32)
    lat_row = 2 * (position // LONP)[None, :] + (cell // 2)[:, None]
    nlat = 2 * PROW_DEV * lax.axis_size("space")
    cell_weight = jnp.cos(math.pi / 2.0 * (lat_row.astype(jnp.float32) + 0.5) / nlat)
    land = lax.dynamic_slice_in_dim(land_mask, x * half, half, 1).astype(jnp.float32)
    valid = jnp.where(kind == 0, 1.0, jnp.where(kind == 1, land[None], 1.0 - land[None]))
    masked = cell_weight[None] * valid

    pre_one = mix(toks, w_one, (1, 0))
    hidden_one = bent(pre_one)
    pre_two = mix(hidden_one, w_two, (1, 0))
    hidden_two = bent(pre_two)
    predicted = mix(w_head, hidden_two, (1, 1))
    error = predicted.reshape(kinds, PP, half) - goal.astype(jnp.float32)
    scored = masked * error
    sums = jnp.stack([jnp.sum(scored * error, axis=(1, 2)), jnp.sum(masked, axis=(1, 2))])
    wide = -(-kinds // 128) * 128
    sums = total(jnp.pad(sums, ((0, 6), (0, wide - kinds))))
    weight_sum = sums[1, :kinds]
    root = jnp.sqrt(sums[0, :kinds] / weight_sum + 1e-06)
    loss = jnp.sum(root) / kinds
    coef = loss_scale / (kinds * root * weight_sum)
    grad_pred = (coef[:, None, None] * scored).reshape(kinds * PP, half).astype(low)

    head_term = mix(hidden_two, grad_pred, (0, 1)).astype(low)
    pad = jnp.zeros((head_term.shape[0], -rows % 128), low)
    head_term = jnp.concatenate([head_term[:, :rows], pad, head_term[:, rows:], pad], axis=1)
    grad_two = (mix(grad_pred, w_head, (0, 0)) * slope(pre_two)).astype(low)
    second_term = mix(hidden_one, grad_two, (0, 0)).astype(low)
    grad_one = (mix(grad_two, w_two, (1, 1)) * slope(pre_one)).astype(low)
    first_term = mix(toks, grad_one, (0, 0)).astype(low)
    token_term = mix(grad_one, w_one, (1, 1)).astype(low)
    first_grad, second_grad, head_grad, arrived = scatter(
        first_term, second_term, head_term, token_term
    )
    kept = lax.dynamic_slice_in_dim(token_term, x * width, width, 1)
    side = lax.broadcasted_iota(jnp.int32, (2, half, width), 0)
    token_grad = jnp.where(side == x, kept[None], arrived[None]).astype(jnp.float32)
    token_grad = token_grad.reshape(count, width)
    return (loss, token_grad, first_grad, second_grad, head_grad[:, :rows].T)


def column_folder(weights, piece):
    return lax.dot_general(
        piece, weights, (((1,), (1,)), ((), ())), preferred_element_type=jnp.float32
    )


def row_folder(weights, piece):
    return lax.dot_general(
        piece, weights, (((0,), (0,)), ((), ())), preferred_element_type=jnp.float32
    )


def per_device_wide(
    tokens, first_weight, second_weight, head_weight, targets, land_mask, variable_kind, loss_scale
):
    count = tokens.shape[0]
    width = first_weight.shape[1]
    kinds = head_weight.shape[0] // PP
    rows_first, rows_second = (
        lax.all_to_all(first_weight, "tensor", split_axis=0, concat_axis=1, tiled=True),
        lax.all_to_all(second_weight, "tensor", split_axis=0, concat_axis=1, tiled=True),
    )
    head_cols = lax.all_to_all(head_weight, "tensor", split_axis=1, concat_axis=0, tiled=True)
    position = lax.axis_index("space") * count + jnp.arange(count, dtype=jnp.int32)
    cell = jnp.arange(PP, dtype=jnp.int32)
    lat_row = 2 * (position // LONP)[None, :] + (cell // 2)[:, None]
    nlat = 2 * PROW_DEV * lax.axis_size("space")
    cell_weight = jnp.cos(math.pi / 2.0 * (lat_row.astype(jnp.float32) + 0.5) / nlat)
    land = land_mask.astype(jnp.float32)
    kind = variable_kind[:, None, None]
    valid = jnp.where(kind == 0, 1.0, jnp.where(kind == 1, land[None], 1.0 - land[None]))
    masked = cell_weight[None] * valid
    local_weight = jnp.sum(masked, axis=(1, 2))
    weight_sum = lax.psum(local_weight, "space")
    full_in = lax.all_gather(tokens, "tensor", axis=1, tiled=True)
    pre_one = jnp.dot(full_in, first_weight, preferred_element_type=jnp.float32)
    hidden_one = jax.nn.gelu(pre_one, approximate=False).astype(jnp.bfloat16)
    full_one = lax.all_gather(hidden_one, "tensor", axis=1, tiled=True)
    pre_two = jnp.dot(full_one, second_weight, preferred_element_type=jnp.float32)
    hidden_two = jax.nn.gelu(pre_two, approximate=False).astype(jnp.bfloat16)
    full_two = lax.all_gather(hidden_two, "tensor", axis=1, tiled=True)
    predicted = lax.dot_general(
        head_weight, full_two, (((1,), (1,)), ((), ())), preferred_element_type=jnp.float32
    )
    error = predicted.reshape(kinds, PP, count) - targets.reshape(kinds, PP, count)
    local_error = jnp.sum(masked * error * error, axis=(1, 2))
    error_sum = lax.psum(local_error, "space")
    root = jnp.sqrt(error_sum / weight_sum + 1e-06)
    loss = lax.psum(jnp.sum(root), "tensor") / (kinds * lax.axis_size("tensor"))
    coef = loss_scale / (kinds * lax.axis_size("tensor") * root * weight_sum)
    grad_pred = (
        (coef[:, None, None] * masked * error).reshape(kinds * PP, count).astype(jnp.bfloat16)
    )
    back_two = row_folder(head_cols, lax.all_gather(grad_pred, "tensor", axis=0, tiled=True))
    head_term = jnp.dot(grad_pred, full_two, preferred_element_type=jnp.float32)
    head_grad = lax.psum_scatter(head_term, "space", scatter_dimension=1, tiled=True)
    grad_two = (back_two * slope(pre_two)).astype(jnp.bfloat16)
    back_one = column_folder(rows_second, lax.all_gather(grad_two, "tensor", axis=1, tiled=True))
    grad_one = (back_one * slope(pre_one)).astype(jnp.bfloat16)
    joined = lax.psum_scatter(
        jnp.concatenate(
            [
                lax.dot_general(
                    full_one, grad_two, (((0,), (0,)), ((), ())), preferred_element_type=jnp.float32
                ),
                lax.dot_general(
                    full_in, grad_one, (((0,), (0,)), ((), ())), preferred_element_type=jnp.float32
                ),
            ],
            axis=1,
        ),
        "space",
        scatter_dimension=0,
        tiled=True,
    )
    second_grad = joined[:, :width]
    first_grad = joined[:, width:]
    token_grad = column_folder(rows_first, lax.all_gather(grad_one, "tensor", axis=1, tiled=True))
    return (loss, token_grad, first_grad, second_grad, head_grad)


def solution(mesh):
    size = mesh.shape["space"]
    paired = mesh.shape["tensor"] == 2 and size >= 8 and size & (size - 1) == 0
    return jax.shard_map(
        per_device if paired else per_device_wide,
        mesh=mesh,
        in_specs=(
            P("space", "tensor"),
            P(None, "tensor"),
            P(None, "tensor"),
            P("tensor", None),
            P("tensor", "space"),
            P(None, "space"),
            P("tensor"),
            P(),
        ),
        out_specs=(
            P(),
            P("space", "tensor"),
            P("space", "tensor"),
            P("space", "tensor"),
            P("tensor", "space"),
        ),
        check_vma=False,
    )
```

profile of v0, /device:TPU:0, one launch (start us, length us, event | category | flops | bytes accessed | tf_op | source)
XLA Modules:
  0.0 105.9 jit_solution(15226293181727636495)
XLA Ops:
  0.7 1.6 %broadcast_subtract_fusion = (f32[4,448]{1,0:T(4,128)S(1)}, f32[4,448]{1,0:T(4,128)S(1)}, f32[4,448]{1,0:T(4,128)}) fusion(s32[4,896]{1,0:T(4,128)} %param.13, s32[]{:T(128)S(6)} %select_n.39, s32[4]{0:T(128)S(1)} %and_select_fusion, s32[448]{0:T(512)S(1)} %fusion.17), kind=kLoop, calls=%fused_computation.45 | loop fusion | flops 10752 | bytes 30484 | tf_op jit(solution)/shard_map/sub | solution.py:413
  2.3 1.1 %convert.9 = bf16[176,896]{1,0:T(8,128)(2,1)S(1)} convert(f32[176,896]{1,0:T(8,128)} %param.12) | non-fusion elementwise | flops 157696 | bytes 946176 | tf_op jit(solution)/shard_map/convert.6
  3.4 0.1 slice_bitcast_fusion.1
  3.5 0.7 convert_element_type.66
  4.2 0.1 broadcast_in_dim.76
  4.3 0.1 convert_element_type.67
  4.4 0.1 broadcast_in_dim.77
  4.5 0.1 pad_maximum_fusion.1.tar
  4.6 0.0 copy-start.2
  4.6 1.2 %copy-done.2 = bf16[896,512]{1,0:T(8,128)(2,1)S(1)} copy-done((bf16[896,512]{1,0:T(8,128)(2,1)S(1)}, bf16[896,512]{1,0:T(8,128)(2,1)}, u32[]{:S(2)}) %copy-start.2) | copy-done | bytes 917528
  5.8 25.8 %gather.1 = (bf16[448,1024]{1,0:T(8,128)(2,1)S(1)}, bf16[1024,1024]{1,0:T(8,128)(2,1)S(1)}, bf16[1024,1024]{1,0:T(8,128)(2,1)S(1)}, bf16[2,176,1024]{2,1,0:T(8,128)(2,1)S(1)}, bf16[2,176,512]{2,1,0:T(8,128)(2,1)S(1)}) custom-call(bf16[896,512]{1,0:T(8,128)(2,1)S(1)} %copy-done.2, bf16[1024,512]{1,0:T(8,128)(2,1)S(1)} %copy-done, ...), custom_call_target="tpu_custom_call" | custom-call | tf_op jit(solution)/shard_map/gather/pallas_call | solution.py:151
  31.6 0.0 copy-start.4
  31.7 2.9 %multiply_convert_fusion.1 = (bf16[448,1024]{1,0:T(8,128)(2,1)S(1)}, f32[448,1024]{1,0:T(8,128)}) fusion(bf16[448,1024]{1,0:T(8,128)(2,1)S(1)} %get-tuple-element.16, bf16[1024,1024]{1,0:T(8,128)(2,1)S(1)} %get-tuple-element.17), kind=kOutput, calls=%fused_computation.18 | convolution fusion | flops 941817856 | bytes 5767168 | tf_op jit(solution)/shard_map/dot_general | solution.py:383
  34.6 2.8 %multiply_convert_fusion = (bf16[448,1024]{1,0:T(8,128)(2,1)}, f32[448,1024]{1,0:T(8,128)}) fusion(bf16[448,1024]{1,0:T(8,128)(2,1)S(1)} %get-tuple-element.35, bf16[1024,1024]{1,0:T(8,128)(2,1)S(1)} %get-tuple-element.18), kind=kOutput, calls=%fused_computation.16 | convolution fusion | flops 941817856 | bytes 5767168 | tf_op jit(solution)/shard_map/dot_general | solution.py:383
  37.4 0.3 compare_reduce_fusion.1
  37.7 0.1 eq.37
  37.8 0.1 copy.18
  37.9 0.1 eq.40
  38.0 0.1 copy.19
  38.1 0.1 slice_convert_fusion
  38.2 0.2 reshape.144
  38.5 0.3 dot_general.29
  38.7 0.1 copy-done.10
  38.8 2.1 %multiply_reduce_fusion = (f32[88]{0:T(128)S(1)}, f32[88]{0:T(128)S(1)}, f32[88,4,448]{2,0,1:T(8,128)S(1)}) fusion(f32[4,448]{1,0:T(4,128)S(1)} %get-tuple-element.29, f32[4,448]{1,0:T(4,128)S(1)} %get-tuple-element.30, f32[4,448]{1,0:T(4,128)S(1)} %copy-done.10, pred[88,4]{0,1:T(4,128)(4,1)S(1)} %copy.19, pred[88,4]{0,1:T(4,128)(4,1)S(1)} %copy.18, ...), kind=kOutput, calls=%fused_computation.29 | convolution fusion | flops 324222784 | bytes 2922880 | tf_op jit(solution)/shard_map/dot_general | solution.py:383
  41.0 10.0 %total.1 = f32[8,128]{1,0:T(8,128)S(1)} custom-call(f32[8,128]{1,0:T(8,128)S(1)} %select_maximum_fusion.v_ref), custom_call_target="tpu_custom_call" | custom-call | tf_op jit(solution)/shard_map/total/pallas_call | solution.py:216
  51.6 0.3 multiply_convert_fusion.2
  51.9 0.2 copy.22
  52.1 0.2 convert_element_type.74
  52.3 0.0 copy-start.12
  52.3 3.8 %fusion.5 = bf16[448,1024]{1,0:T(8,128)(2,1)} fusion(f32[448,1024]{1,0:T(8,128)} %get-tuple-element.38, bf16[352,448]{1,0:T(8,128)(2,1)S(1)} %convert_element_type.74, bf16[352,1024]{1,0:T(8,128)(2,1)S(1)} %bitcast.55), kind=kOutput, calls=%fused_computation.9 | convolution fusion | flops 327548928 | bytes 3788800 | tf_op jit(solution)/shard_map/dot_general | solution.py:383
  56.1 3.1 %fusion.11 = bf16[448,1024]{1,0:T(8,128)(2,1)S(1)} fusion(f32[448,1024]{1,0:T(8,128)S(1)} %copy-done.12, bf16[448,1024]{1,0:T(8,128)(2,1)} %fusion.5, bf16[1024,1024]{1,0:T(8,128)(2,1)S(1)} %copy-done.7), kind=kOutput, calls=%fused_computation.15 | convolution fusion | flops 944111616 | bytes 5767168 | tf_op jit(solution)/shard_map/dot_general | solution.py:383
  59.2 0.0 copy-start.14
  59.2 1.2 %convolution_convert_fusion.2.refs_3_ = bf16[448,1024]{1,0:T(8,128)(2,1)S(1)} fusion(bf16[448,1024]{1,0:T(8,128)(2,1)S(1)} %fusion.11, bf16[1024,1024]{1,0:T(8,128)(2,1)S(1)} %copy-done.5), kind=kOutput, calls=%fused_computation.20 | convolution fusion | flops 939982848 | bytes 3932160 | tf_op jit(solution)/shard_map/dot_general | solution.py:383
  60.4 0.3 copy-done.11
  60.7 0.5 convolution_convert_fusion.3
  61.3 0.1 pad_maximum_fusion
  61.4 0.5 copy.23
  62.0 0.0 copy-start.15
  62.0 2.9 %convolution_convert_fusion = bf16[1024,1024]{1,0:T(8,128)(2,1)S(1)} fusion(bf16[448,1024]{1,0:T(8,128)(2,1)} %copy-done.13, bf16[448,1024]{1,0:T(8,128)(2,1)} %fusion.5), kind=kOutput, calls=%fused_computation.2 | convolution fusion | flops 940572672 | bytes 3932160 | tf_op jit(solution)/shard_map/dot_general | solution.py:383
  64.9 1.3 %convolution_convert_fusion.1 = bf16[1024,1024]{1,0:T(8,128)(2,1)S(1)} fusion(bf16[448,1024]{1,0:T(8,128)(2,1)S(1)} %copy-done.9, bf16[448,1024]{1,0:T(8,128)(2,1)S(1)} %copy-done.15), kind=kOutput, calls=%fused_computation.3 | convolution fusion | flops 940572672 | bytes 3932160 | tf_op jit(solution)/shard_map/dot_general | solution.py:383
  66.2 33.6 %scatter.1 = (f32[64,512]{1,0:T(8,128)S(1)}, f32[64,512]{1,0:T(8,128)S(1)}, f32[64,256]{1,0:T(8,128)S(1)}, bf16[448,512]{1,0:T(8,128)(2,1)S(1)}) custom-call(bf16[2,2,2,2,64,1024]{5,4,3,2,1,0:T(8,128)(2,1)S(1)} %bitcast.54, bf16[2,2,2,2,64,1024]{5,4,3,2,1,0:T(8,128)(2,1)S(1)} %bitcast.53, bf16[2,2,2,2,64,512]{5,4,3,2,1,0:T(8,128)(2,1)S(1)} %bitcast.52, ...), custom_call_target="tpu_custom_call" | custom-call | tf_op jit(solution)/shard_map/scatter/pallas_call | solution.py:369
  99.9 0.1 iota.23
  100.0 0.1 iota.24
  100.1 1.4 %fusion.12 = f32[896,512]{1,0:T(8,128)} fusion(pred[896]{0:T(1024)(128)(4,1)S(1)} %iota.24, bf16[448,512]{1,0:T(8,128)(2,1)S(1)} %get-tuple-element.19, bf16[448,512]{1,0:T(8,128)(2,1)S(1)} %constant_dynamic-slice_fusion), kind=kLoop, calls=%fused_computation.25 | loop fusion | flops 917504 | bytes 2753408 | tf_op jit(solution)/shard_map/convert_element_type | solution.py:445
  101.5 0.6 slice_bitcast_fusion.2
  102.2 0.6 reduce_sum.29
  103.4 0.7 copy.32
  104.1 0.7 copy.33
  (32 shorter events, 0.2 us)
Async XLA Ops:
  0.6 4.0 %copy-start.1 = (bf16[1024,512]{1,0:T(8,128)(2,1)S(1)}, bf16[1024,512]{1,0:T(8,128)(2,1)}, u32[]{:S(2)}) copy-start(bf16[1024,512]{1,0:T(8,128)(2,1)} %two.1) | copy-start | bytes 3145732
  0.6 4.0 %copy-start.3 = (bf16[176,1024]{1,0:T(8,128)(2,1)S(1)}, bf16[176,1024]{1,0:T(8,128)(2,1)}, u32[]{:S(2)}) copy-start(bf16[176,1024]{1,0:T(8,128)(2,1)} %head.1) | copy-start | bytes 1081348
  0.7 4.0 %copy-start = (bf16[1024,512]{1,0:T(8,128)(2,1)S(1)}, bf16[1024,512]{1,0:T(8,128)(2,1)}, u32[]{:S(2)}) copy-start(bf16[1024,512]{1,0:T(8,128)(2,1)} %one.1) | copy-start | bytes 3145732
  4.6 1.2 %copy-start.2 = (bf16[896,512]{1,0:T(8,128)(2,1)S(1)}, bf16[896,512]{1,0:T(8,128)(2,1)}, u32[]{:S(2)}) copy-start(bf16[896,512]{1,0:T(8,128)(2,1)} %tok.1) | copy-start | bytes 2752516
  31.6 2.9 %copy-start.4 = (bf16[1024,1024]{1,0:T(8,128)(2,1)}, bf16[1024,1024]{1,0:T(8,128)(2,1)S(1)}, u32[]{:S(2)}) copy-start(bf16[1024,1024]{1,0:T(8,128)(2,1)S(1)} %get-tuple-element.17) | copy-start | bytes 6291460
  31.7 2.9 %copy-start.8 = (bf16[448,1024]{1,0:T(8,128)(2,1)}, bf16[448,1024]{1,0:T(8,128)(2,1)S(1)}, u32[]{:S(2)}) copy-start(bf16[448,1024]{1,0:T(8,128)(2,1)S(1)} %get-tuple-element.16) | copy-start | bytes 2752516
  31.7 2.9 %copy-start.6 = (bf16[1024,1024]{1,0:T(8,128)(2,1)}, bf16[1024,1024]{1,0:T(8,128)(2,1)S(1)}, u32[]{:S(2)}) copy-start(bf16[1024,1024]{1,0:T(8,128)(2,1)S(1)} %get-tuple-element.18) | copy-start | bytes 6291460
  34.6 3.1 %copy-start.13 = (bf16[448,1024]{1,0:T(8,128)(2,1)}, bf16[448,1024]{1,0:T(8,128)(2,1)S(1)}, u32[]{:S(2)}) copy-start(bf16[448,1024]{1,0:T(8,128)(2,1)S(1)} %get-tuple-element.35) | copy-start | bytes 2752516
  38.1 0.7 copy-start.10
  52.3 3.8 %copy-start.7 = (bf16[1024,1024]{1,0:T(8,128)(2,1)S(1)}, bf16[1024,1024]{1,0:T(8,128)(2,1)}, u32[]{:S(2)}) copy-start(bf16[1024,1024]{1,0:T(8,128)(2,1)} %copy-done.6) | copy-start | bytes 6291460
  52.3 3.8 %copy-start.12 = (f32[448,1024]{1,0:T(8,128)S(1)}, f32[448,1024]{1,0:T(8,128)}, u32[]{:S(2)}) copy-start(f32[448,1024]{1,0:T(8,128)} %get-tuple-element.36) | copy-start | bytes 5505028
  56.1 3.1 %copy-start.5 = (bf16[1024,1024]{1,0:T(8,128)(2,1)S(1)}, bf16[1024,1024]{1,0:T(8,128)(2,1)}, u32[]{:S(2)}) copy-start(bf16[1024,1024]{1,0:T(8,128)(2,1)} %copy-done.4) | copy-start | bytes 6291460
  59.2 1.2 %copy-start.14 = (bf16[448,1024]{1,0:T(8,128)(2,1)}, bf16[448,1024]{1,0:T(8,128)(2,1)S(1)}, u32[]{:S(2)}) copy-start(bf16[448,1024]{1,0:T(8,128)(2,1)S(1)} %fusion.11) | copy-start | bytes 2752516
  59.2 1.5 %copy-start.11 = (bf16[448,1024]{1,0:T(8,128)(2,1)S(1)}, bf16[448,1024]{1,0:T(8,128)(2,1)}, u32[]{:S(2)}) copy-start(bf16[448,1024]{1,0:T(8,128)(2,1)} %get-tuple-element.37) | copy-start | bytes 2752516
  62.0 2.9 %copy-start.9 = (bf16[448,1024]{1,0:T(8,128)(2,1)S(1)}, bf16[448,1024]{1,0:T(8,128)(2,1)}, u32[]{:S(2)}) copy-start(bf16[448,1024]{1,0:T(8,128)(2,1)} %copy-done.8) | copy-start | bytes 2752516
  62.0 2.9 %copy-start.15 = (bf16[448,1024]{1,0:T(8,128)(2,1)S(1)}, bf16[448,1024]{1,0:T(8,128)(2,1)}, u32[]{:S(2)}) copy-start(bf16[448,1024]{1,0:T(8,128)(2,1)} %copy-done.14) | copy-start | bytes 2752516
where the time goes:
time: 106 us
  Pallas kernels  69.4 us (65%)
  matrix products  20.5 us (19%)
  other arithmetic  6.32 us (6%)
  local copies, waits for them, and re-layouts  6.11 us (6%)
  between operations  3.46 us (3%)
    pallas_call x1, Pallas kernels, scatter(): pl.pallas_call(functools.partial(scatter_kernel, bits, plan), out_shape=t...  33.6 us
    pallas_call x1, Pallas kernels, gather(): pl.pallas_call(gather_kernel, out_shape=(shape((half, 2 * width), tokens....  25.8 us
    dot_general x9, matrix products, mix(): lax.dot_general(a, b, ((dims[:1], dims[1:]), ((), ())), preferred_element...  20.5 us
    pallas_call x1, Pallas kernels, total(): pl.pallas_call(functools.partial(total_kernel, groups), out_shape=jax.Sha...  9.99 us
    unnamed x34, local copies, waits for them, and re-layouts  2.97 us

commit v1 on v0

v1 whole, which is shorter than its diff:
```python
import math

import jax
import jax.numpy as jnp
from jax import lax
from jax.experimental import pallas as pl
from jax.experimental.pallas import tpu as pltpu
from jax.sharding import PartitionSpec as P

PP = 4
PROW_DEV = 4
LONP = 224
MESH = pl.DeviceIdType.MESH
VMEM = pl.BlockSpec(memory_space=pltpu.VMEM)
ANY = pl.BlockSpec(memory_space=pl.ANY)


def bent(z):
    return (0.5 * z * (1.0 + lax.erf(z / math.sqrt(2.0)))).astype(jnp.bfloat16)


def slope(z):
    cdf = 0.5 * (1.0 + lax.erf(z / math.sqrt(2.0)))
    return cdf + z * jnp.exp(-0.5 * z * z) / math.sqrt(2.0 * math.pi)


def flipped(s, bit):
    step = 1 << bit
    return s + step - 2 * step * ((s // step) % 2)


def greet(partners):
    barrier = pltpu.get_barrier_semaphore()
    for partner in partners:
        pl.semaphore_signal(barrier, inc=1, device_id=partner, device_id_type=MESH)
    pl.semaphore_wait(barrier, len(partners))


def params(number, mib):
    return pltpu.CompilerParams(
        collective_id=number, has_side_effects=True, vmem_limit_bytes=mib * 2**20
    )


TILE = 128
RELAYS = (
    (0, 0), (1, 0), (2, 0), (0, 8), (0, 4), (1, 8), (0, 2), (2, 8), (1, 4), (0, 12), (2, 4),
    (0, 10), (1, 2), (1, 12), (2, 2), (2, 12), (0, 6), (0, 14),
)
CORE_SIDE = (1, 9, 5, 13, 3, 11, 7, 15)
PLAN = ("y", "y", "z", "y", "z")


def fused_kernel(
    scale, label, land, tok, one, two, head, tar,
    o_loss, o_tok, o_one, o_two, o_head,
    w_one, w_two, w_head, toks, tok_out, tar_v, tar_s, tar_all, lnd, masked,
    pre_one, pre_two, h_one, h_two, t_tok, t_one, t_two, tgt, scored, sc_low, sc_par, gp_low,
    g_two, g_one, p_two, p_one, tg_out, hb,
    msg, near, far, mid,
    fars, arrs0, nears0, fars1, arrs1, nears1, fars2, arrs2, nears2, finals, arrs3, arrs4, arrs5,
    local, wsend, wrecv, xsend, xrecv, dsend, drecv, tsend, trecv, rsend, rrecv,
):
    low, wide = jnp.bfloat16, jnp.float32
    s, x = lax.axis_index("space"), lax.axis_index("tensor")
    other = 1 - x
    zf, zn, yy, core = (s // 8) % 2, (s // 4) % 2, (s // 2) % 2, s % 2
    oc = 1 - core
    count = tok.shape[0]
    half = count // 2
    dim, width = one.shape
    rows = head.shape[0]
    pad = toks.shape[0]
    vw = 2 * TILE
    hr = TILE // 2
    across, partner = (s, other), (flipped(s, 0), x)
    diagonal = (flipped(flipped(s, 3), 0), x)
    started = []

    def at(index, size, base=0):
        return pl.ds(pl.multiple_of(index * size + base, math.gcd(size, base) if base else size), size)

    def remote(src, dst, sends, recvs, slot, target):
        copy = pltpu.make_async_remote_copy(
            src_ref=src,
            dst_ref=dst,
            send_sem=sends.at[slot],
            recv_sem=recvs.at[slot],
            device_id=target,
            device_id_type=MESH,
        )
        copy.start()
        started.append(copy)
        return copy

    moves = [
        (one, w_one.at[:, at(x, width)]),
        (two, w_two.at[:, at(x, width)]),
        (head, w_head.at[pl.ds(pl.multiple_of(x * vw, vw), rows), :]),
        (tok.at[at(other, half), :], tok_out),
        (tar, tar_v),
        (tok.at[at(x, half), :], toks.at[pl.ds(0, half), at(x, width)]),
    ]
    loads = [pltpu.make_async_copy(a, b, local.at[n]) for n, (a, b) in enumerate(moves)]
    for copy in loads:
        copy.start()

    shard = 96
    w_head[pl.ds(pl.multiple_of(x * vw + rows, 16), vw - rows), :] = jnp.zeros((vw - rows, dim), low)
    w_head[pl.ds(pl.multiple_of(other * vw + 2 * shard, 16), vw - 2 * shard), :] = jnp.zeros(
        (vw - 2 * shard, dim), low
    )
    for ref in (toks, h_one, h_two, g_two, g_one, sc_low):
        ref[half:, :] = jnp.zeros((pad - half, ref.shape[1]), low)
    tar_all[:, rows:, :] = jnp.zeros((2, vw - rows, pad), low)

    low_bits, high = s % 4, s // 4
    mine = x * 4 + low_bits

    def near_peer(d):
        j = (mine + d) % 8
        return (high * 4 + j % 4, j // 4)

    def far_peer(d):
        return (((high + d) % 4) * 4 + low_bits, x)

    greet([near_peer(d) for d in range(1, 8)] + [far_peer(d) for d in range(1, 4)] + [diagonal])

    part = dim // 16

    def place(k, m, side):
        q = s
        for b in range(4):
            if (m >> b) & 1:
                q = flipped(q, b)
        if k < 2:
            return (w_one, w_two)[k].at[at(q, part), at(side, width)]
        first = pl.multiple_of(side * vw + (q % 2) * shard, 16)
        return w_head.at[pl.ds(first, shard), at(q // 2, TILE)]

    pieces = {}
    for k in range(3):
        loads[k].wait()
        pieces[k, 0] = remote(place(k, 0, x), place(k, 0, x), wsend, wrecv, 16 * k, across)
    loads[3].wait()
    parts = 2
    step = half // parts
    tok_copies = [
        remote(
            tok_out.at[pl.ds(n * step, step), :],
            toks.at[pl.ds(n * step, step), at(x, width)],
            xsend, xrecv, n, across,
        )
        for n in range(parts)
    ]
    loads[4].wait()
    tail = count - pad
    spare = lax.broadcasted_iota(jnp.int32, (rows, pad), 1) >= half
    tags = jnp.concatenate([label[...]] * (pad // TILE), axis=1)
    lo = tar_v[:, :pad]
    hi = pltpu.roll(tar_v[:, tail:], pad - half + tail, 1)
    tar_s[...] = jnp.where(spare, tags, jnp.where(x == 0, hi, lo)).astype(low)
    tar_copy = remote(tar_s, tar_all.at[x, pl.ds(0, rows), :], xsend, xrecv, parts, across)
    tar_all[x, 0:rows, :] = jnp.where(spare, tags, jnp.where(x == 0, lo, hi)).astype(low)
    loads[5].wait()

    def relay(k, m):
        pieces[k, m].wait_recv()
        for b in (3, 2, 1, 0):
            if m & ((2 << b) - 1) == 0:
                piece = place(k, m, other)
                new = m ^ (1 << b)
                pieces[k, new] = remote(piece, piece, wsend, wrecv, 16 * k + new, (flipped(s, b), x))

    for k, m in RELAYS:
        relay(k, m)
    for m in CORE_SIDE:
        relay(0, m)

    def one_rows(first, size):
        def body(n, _):
            z = jnp.dot(toks[first : first + size, :], w_one[:, at(n, vw)], preferred_element_type=wide)
            pre_one[first : first + size, at(n, vw)] = z
            h_one[first : first + size, at(n, vw)] = bent(z)
            return 0

        lax.fori_loop(0, dim // vw, body, 0)

    for n in range(parts):
        tok_copies[n].wait_recv()
        one_rows(n * step, step)
    for k, m in ((1, 10), (2, 10), (1, 6), (1, 14), (2, 6), (2, 14)):
        relay(k, m)
    for m in CORE_SIDE:
        relay(1, m)

    def two_body(n, _):
        z = jnp.dot(h_one[0:half, :], w_two[:, at(n, vw)], preferred_element_type=wide)
        pre_two[:, at(n, vw)] = z
        h_two[0:half, at(n, vw)] = bent(z)
        return 0

    lax.fori_loop(0, dim // vw, two_body, 0)
    for m in CORE_SIDE:
        relay(2, m)
    tar_copy.wait_recv()

    for side in range(2):
        tgt[:, side * vw : (side + 1) * vw] = tar_all[side].astype(wide).T
    lane = lax.broadcasted_iota(jnp.int32, (1, 2 * vw), 1)
    used = lane % vw < rows
    kind = tgt[half : half + 1, :]
    cell = lane % PP
    lnd[...] = jnp.zeros_like(lnd)
    lnd[0:PP, :] = land[...].astype(wide)
    ground = jnp.where(x == 0, lnd[:, :pad], pltpu.roll(lnd[:, tail:], pad - half + tail, 1))
    pick_shape = (TILE, 2 * vw)
    pick = lax.broadcasted_iota(jnp.int32, pick_shape, 1) % PP == lax.broadcasted_iota(jnp.int32, pick_shape, 0)
    spread = jnp.dot(
        ground.T.astype(low), jnp.where(pick, 1.0, 0.0).astype(low), preferred_element_type=wide
    )
    bands = half // LONP
    nlat = 2 * (count // LONP) * lax.axis_size("space")
    for j in range(bands):
        lat_row = 2 * (s * (count // LONP) + x * bands + j) + cell // 2
        weight = jnp.cos(math.pi / 2.0 * (lat_row.astype(wide) + 0.5) / nlat)
        weight = jnp.where(used, weight, 0.0)
        flat = jnp.where(kind == 1.0, 0.0, weight)
        slant = jnp.where(kind == 1.0, weight, jnp.where(kind == 2.0, -weight, 0.0))
        band = slice(j * LONP, (j + 1) * LONP)
        masked[band, :] = flat + slant * spread[band, :]

    for side in range(2):
        cols = slice(side * vw, (side + 1) * vw)
        error = lax.dot_general(
            h_two[0:half, :], w_head[cols, :], (((1,), (1,)), ((), ())), preferred_element_type=wide
        )
        error = error - tgt[0:half, cols]
        m = masked[:, cols]
        sc = m * error
        scored[:, cols] = sc
        sc_low[0:half, cols] = sc.astype(low)
        esum = jnp.sum(sc * error, axis=0, keepdims=True)
        wsum = jnp.sum(m, axis=0, keepdims=True)
        for n in range(2):
            r = side * 2 + n
            msg[r : r + 1, :] = esum[:, n * TILE : (n + 1) * TILE]
            msg[4 + r : 5 + r, :] = wsum[:, n * TILE : (n + 1) * TILE]

    def share(src, slots, me, peers, base):
        copies = [remote(src, slots.at[me], tsend, trecv, base + n, peer) for n, peer in enumerate(peers)]
        slots[me] = src[...]
        return copies

    first_share = share(msg, near, mine, [near_peer(d) for d in range(1, 8)], 0)

    def scored_cols(side, c):
        return pl.ds(pl.multiple_of(side * vw + c * TILE, TILE), TILE)

    score_copies = [
        remote(sc_low.at[:, scored_cols(n, oc)], sc_par.at[:, pl.ds(n * TILE, TILE)], dsend, drecv, n, partner)
        for n in range(2)
    ]

    def flip_to(src, dst, slot):
        def body(n, _):
            dst[0, at(n, TILE), :] = src[:, at(n, TILE)].T
            return 0

        lax.fori_loop(0, dim // TILE, body, 0)
        return remote(dst.at[0], dst.at[1], dsend, drecv, slot, partner)

    flips = [flip_to(h_two, t_two, 2)]
    for copy in first_share:
        copy.wait_recv()
    mid[...] = jnp.sum(near[...], axis=0)
    second_share = share(mid, far, high, [far_peer(d) for d in range(1, 4)], 7)
    flips += [flip_to(h_one, t_one, 3), flip_to(toks, t_tok, 4)]

    def make_slope(ref):
        def body(n, _):
            ref[:, at(n, TILE)] = slope(ref[:, at(n, TILE)])
            return 0

        lax.fori_loop(0, dim // TILE, body, 0)

    ways = {"z": (zn, 2), "y": (yy, 1)}

    def produce(g, trans, own_cols, par_cols):
        value, bit = ways[PLAN[g]]

        def product(v):
            def side_rows(k):
                blocks = []
                for i in range(2):
                    for j in range(2):
                        index = i * 4 + (j * 2 + v if PLAN[g] == "y" else v * 2 + j)
                        blocks.append(trans[k, at(index, TILE), :])
                return jnp.concatenate(blocks, axis=0)

            out = jnp.dot(side_rows(0), own_cols, preferred_element_type=wide)
            out += jnp.dot(side_rows(1), par_cols, preferred_element_type=wide)
            return out.reshape(2, 2, TILE, vw)

        fars[g] = product(1 - value).astype(low)
        copy = remote(fars.at[g], arrs0.at[g], rsend, rrecv, 6 * g, (flipped(s, bit), x))
        nears0[g] = product(value)
        return copy

    def advance_one(g, copy):
        copy.wait_recv()
        value, bit = ways["z" if PLAN[g] == "y" else "y"]
        fars1[g] = (nears0[g, :, 1 - value] + arrs0[g, :, 1 - value].astype(wide)).astype(low)
        copy = remote(fars1.at[g], arrs1.at[g], rsend, rrecv, 6 * g + 1, (flipped(s, bit), x))
        nears1[g] = nears0[g, :, value] + arrs0[g, :, value].astype(wide)
        return copy

    def advance_two(g, copy):
        copy.wait_recv()
        away, here = at(other, TILE), at(x, TILE)
        fars2[g] = (nears1[g, :, :, away] + arrs1[g, :, :, away].astype(wide)).astype(low)
        copy = remote(fars2.at[g], arrs2.at[g], rsend, rrecv, 6 * g + 2, across)
        nears2[g] = nears1[g, :, :, here] + arrs1[g, :, :, here].astype(wide)
        return copy

    def advance_three(g, copy):
        copy.wait_recv()
        finals[g] = (nears2[g, 1 - zf] + arrs2[g, 1 - zf].astype(wide)).astype(low)
        up = (flipped(s, 3), x)
        copies = [
            remote(finals.at[g, at(core, hr), :], arrs4.at[g], rsend, rrecv, 6 * g + 3, up),
            remote(finals.at[g, at(oc, hr), :], arrs5.at[g], rsend, rrecv, 6 * g + 4, diagonal),
        ]
        nears2[g, zf] = nears2[g, zf] + arrs2[g, zf].astype(wide)
        copies.append(
            remote(nears2.at[g, zf, at(oc, hr), :], arrs3.at[g], rsend, rrecv, 6 * g + 5, partner)
        )
        return copies

    def finish(g, copies, out, base):
        for copy in copies:
            copy.wait_recv()
        kept = nears2[g, zf, at(core, hr), :] + arrs4[g].astype(wide)
        came = arrs3[g] + arrs5[g].astype(wide)
        span = out.shape[1] // 2
        out[pl.ds(0, hr), pl.ds(pl.multiple_of(core * span + base, TILE), TILE)] = kept
        out[pl.ds(0, hr), pl.ds(pl.multiple_of(oc * span + base, TILE), TILE)] = came

    for copy in score_copies:
        copy.wait_recv()
    flips[0].wait_recv()
    state = {}
    own = jnp.concatenate([sc_low[:, scored_cols(n, core)] for n in range(2)], axis=1)
    state[0] = produce(0, t_two, own, sc_par[...])
    make_slope(pre_two)

    for copy in second_share:
        copy.wait_recv()
    sums = jnp.sum(far[...], axis=0)
    tl = lax.broadcasted_iota(jnp.int32, (8, TILE), 1)
    sums = sums + jnp.where(tl % 2 == 0, pltpu.roll(sums, TILE - 1, 1), pltpu.roll(sums, 1, 1))
    sums = sums + jnp.where(tl % 4 < 2, pltpu.roll(sums, TILE - 2, 1), pltpu.roll(sums, 2, 1))
    kinds = 2 * rows // PP
    line = lax.broadcasted_iota(jnp.int32, (4, TILE), 0)
    tl = lax.broadcasted_iota(jnp.int32, (4, TILE), 1)
    ok = (line % 2) * TILE + tl < rows
    weight_sum = jnp.where(ok, sums[4:8, :], 1.0)
    root = jnp.sqrt(jnp.where(ok, sums[0:4, :], 0.0) / weight_sum + 1e-06)
    roots = jnp.where(ok & (tl % PP == 0), root, 0.0)
    loss = jnp.sum(jnp.sum(roots, axis=0, keepdims=True), axis=1, keepdims=True) / kinds
    o_loss[...] = jnp.broadcast_to(loss, o_loss.shape)
    coef = jnp.where(ok, scale[0] / (kinds * root * weight_sum), 0.0)
    coef = jnp.concatenate([coef[n : n + 1, :] for n in range(4)], axis=1)
    gp_low[...] = (coef * scored[...]).astype(low)

    def grad_tiles(made, send_to, base, make):
        copies = []
        for c in (oc, core):
            for side in range(2):
                tile = pl.ds(pl.multiple_of(side * width + c * vw, vw), vw)
                made[0:half, tile] = make(tile)
                if c is oc:
                    copies.append(
                        remote(
                            made.at[:, tile], send_to.at[:, pl.ds(side * vw, vw)],
                            dsend, drecv, base + side, partner,
                        )
                    )
        return copies

    def make_two(tile):
        b = jnp.dot(gp_low[...], w_head[:, tile], preferred_element_type=wide)
        return (b * pre_two[:, tile]).astype(low)

    two_copies = grad_tiles(g_two, p_two, 5, make_two)
    make_slope(pre_one)

    def make_one(tile):
        b = lax.dot_general(
            g_two[0:half, :], w_two[tile, :], (((1,), (1,)), ((), ())), preferred_element_type=wide
        )
        return (b * pre_one[:, tile]).astype(low)

    one_copies = grad_tiles(g_one, p_one, 7, make_one)

    def both(made, came, a):
        own_cols = [
            made[:, pl.ds(pl.multiple_of(n * width + core * vw + a * TILE, TILE), TILE)] for n in range(2)
        ]
        par_cols = [came[:, n * vw + a * TILE : n * vw + (a + 1) * TILE] for n in range(2)]
        return jnp.concatenate(own_cols, axis=1), jnp.concatenate(par_cols, axis=1)

    for copy in two_copies + [flips[1]]:
        copy.wait_recv()
    for a in range(2):
        state[1 + a] = produce(1 + a, t_one, *both(g_two, p_two, a))
    state[0] = advance_one(0, state[0])
    for copy in one_copies + [flips[2]]:
        copy.wait_recv()
    for a in range(2):
        state[3 + a] = produce(3 + a, t_tok, *both(g_one, p_one, a))
    state[0] = advance_two(0, state[0])

    def token_side(side, write):
        for n in range(width // vw):
            b = lax.dot_general(
                g_one[0:half, :],
                w_one[pl.ds(pl.multiple_of(side * width + n * vw, vw), vw), :],
                (((1,), (1,)), ((), ())),
                preferred_element_type=wide,
            )
            write(n, b.astype(low))

    def write_far(n, b):
        tg_out[:, n * vw : (n + 1) * vw] = b

    def write_near(n, b):
        o_tok[at(x, half), n * vw : (n + 1) * vw] = b

    token_side(other, write_far)
    tg_copy = remote(tg_out, o_tok.at[at(x, half), :], xsend, xrecv, parts + 1, across)
    state[1] = advance_one(1, state[1])
    state[2] = advance_one(2, state[2])
    token_side(x, write_near)
    state[0] = advance_three(0, state[0])
    state[3] = advance_one(3, state[3])
    state[1] = advance_two(1, state[1])
    state[2] = advance_two(2, state[2])
    state[4] = advance_one(4, state[4])
    finish(0, state[0], hb, 0)
    coef_here = jnp.where(x == 0, coef[:, :vw], coef[:, vw:])
    o_head[...] = (hb[...] * coef_here).T[0:rows, 0:hr]
    state[1] = advance_three(1, state[1])
    state[2] = advance_three(2, state[2])
    state[3] = advance_two(3, state[3])
    state[4] = advance_two(4, state[4])
    finish(1, state[1], o_two, 0)
    finish(2, state[2], o_two, TILE)
    state[3] = advance_three(3, state[3])
    state[4] = advance_three(4, state[4])
    finish(3, state[3], o_one, 0)
    finish(4, state[4], o_one, TILE)
    tg_copy.wait_recv()
    for copy in started:
        copy.wait_send()


def fused(scale, label, land, tokens, first, second, head, targets):
    count, width = tokens.shape
    dim = first.shape[0]
    rows = head.shape[0]
    half = count // 2
    pad = -(-(half + 1) // TILE) * TILE
    vw = 2 * TILE
    hr = TILE // 2
    low, wide = jnp.bfloat16, jnp.float32
    shape = jax.ShapeDtypeStruct
    slices = len(PLAN)
    vm = pltpu.VMEM
    scratch = [
        vm((dim, dim), low), vm((dim, dim), low), vm((2 * vw, dim), low), vm((pad, dim), low),
        vm((half, width), low), vm((rows, count), wide), vm((rows, pad), low), vm((2, vw, pad), low),
        vm((TILE, count), wide), vm((half, 2 * vw), wide),
        vm((half, dim), wide), vm((half, dim), wide), vm((pad, dim), low), vm((pad, dim), low),
        vm((2, dim, pad), low), vm((2, dim, pad), low), vm((2, dim, pad), low),
        vm((pad, 2 * vw), wide), vm((half, 2 * vw), wide), vm((pad, 2 * vw), low), vm((pad, vw), low),
        vm((half, 2 * vw), low),
        vm((pad, dim), low), vm((pad, dim), low), vm((pad, width), low), vm((pad, width), low),
        vm((half, width), low), vm((TILE, vw), wide),
        vm((8, TILE), wide), vm((8, 8, TILE), wide), vm((4, 8, TILE), wide), vm((8, TILE), wide),
        vm((slices, 2, 2, TILE, vw), low), vm((slices, 2, 2, TILE, vw), low), vm((slices, 2, 2, TILE, vw), wide),
        vm((slices, 2, TILE, vw), low), vm((slices, 2, TILE, vw), low), vm((slices, 2, TILE, vw), wide),
        vm((slices, 2, TILE, TILE), low), vm((slices, 2, TILE, TILE), low), vm((slices, 2, TILE, TILE), wide),
        vm((slices, TILE, TILE), low), vm((slices, hr, TILE), wide),
        vm((slices, hr, TILE), low), vm((slices, hr, TILE), low),
    ]
    sizes = (6, 48, 48, 4, 4, 9, 9, 10, 10, 6 * slices, 6 * slices)
    scratch += [pltpu.SemaphoreType.DMA((n,)) for n in sizes]
    return pl.pallas_call(
        fused_kernel,
        out_shape=(
            shape((8, TILE), wide),
            shape((count, width), low),
            shape((dim // 16, width), wide),
            shape((dim // 16, width), wide),
            shape((rows, hr), wide),
        ),
        in_specs=[pl.BlockSpec(memory_space=pltpu.SMEM), VMEM, VMEM] + [ANY] * 5,
        out_specs=[VMEM] * 5,
        scratch_shapes=scratch,
        compiler_params=params(0, 56),
        name="fused",
    )(scale, label, land, tokens, first, second, head, targets)


def per_device(
    tokens, first_weight, second_weight, head_weight, targets, land_mask, variable_kind, loss_scale
):
    rows = head_weight.shape[0]
    label = jnp.repeat(variable_kind, PP).astype(jnp.float32)[:, None]
    label = jnp.broadcast_to(label, (rows, TILE))
    loss, token_grad, first_grad, second_grad, head_grad = fused(
        loss_scale.reshape(1), label, land_mask, tokens, first_weight, second_weight, head_weight, targets
    )
    return (loss[0, 0], token_grad.astype(jnp.float32), first_grad, second_grad, head_grad)


def column_folder(weights, piece):
    return lax.dot_general(
        piece, weights, (((1,), (1,)), ((), ())), preferred_element_type=jnp.float32
    )


def row_folder(weights, piece):
    return lax.dot_general(
        piece, weights, (((0,), (0,)), ((), ())), preferred_element_type=jnp.float32
    )


def per_device_wide(
    tokens, first_weight, second_weight, head_weight, targets, land_mask, variable_kind, loss_scale
):
    count = tokens.shape[0]
    width = first_weight.shape[1]
    kinds = head_weight.shape[0] // PP
    rows_first, rows_second = (
        lax.all_to_all(first_weight, "tensor", split_axis=0, concat_axis=1, tiled=True),
        lax.all_to_all(second_weight, "tensor", split_axis=0, concat_axis=1, tiled=True),
    )
    head_cols = lax.all_to_all(head_weight, "tensor", split_axis=1, concat_axis=0, tiled=True)
    position = lax.axis_index("space") * count + jnp.arange(count, dtype=jnp.int32)
    cell = jnp.arange(PP, dtype=jnp.int32)
    lat_row = 2 * (position // LONP)[None, :] + (cell // 2)[:, None]
    nlat = 2 * PROW_DEV * lax.axis_size("space")
    cell_weight = jnp.cos(math.pi / 2.0 * (lat_row.astype(jnp.float32) + 0.5) / nlat)
    land = land_mask.astype(jnp.float32)
    kind = variable_kind[:, None, None]
    valid = jnp.where(kind == 0, 1.0, jnp.where(kind == 1, land[None], 1.0 - land[None]))
    masked = cell_weight[None] * valid
    local_weight = jnp.sum(masked, axis=(1, 2))
    weight_sum = lax.psum(local_weight, "space")
    full_in = lax.all_gather(tokens, "tensor", axis=1, tiled=True)
    pre_one = jnp.dot(full_in, first_weight, preferred_element_type=jnp.float32)
    hidden_one = jax.nn.gelu(pre_one, approximate=False).astype(jnp.bfloat16)
    full_one = lax.all_gather(hidden_one, "tensor", axis=1, tiled=True)
    pre_two = jnp.dot(full_one, second_weight, preferred_element_type=jnp.float32)
    hidden_two = jax.nn.gelu(pre_two, approximate=False).astype(jnp.bfloat16)
    full_two = lax.all_gather(hidden_two, "tensor", axis=1, tiled=True)
    predicted = lax.dot_general(
        head_weight, full_two, (((1,), (1,)), ((), ())), preferred_element_type=jnp.float32
    )
    error = predicted.reshape(kinds, PP, count) - targets.reshape(kinds, PP, count)
    local_error = jnp.sum(masked * error * error, axis=(1, 2))
    error_sum = lax.psum(local_error, "space")
    root = jnp.sqrt(error_sum / weight_sum + 1e-06)
    loss = lax.psum(jnp.sum(root), "tensor") / (kinds * lax.axis_size("tensor"))
    coef = loss_scale / (kinds * lax.axis_size("tensor") * root * weight_sum)
    grad_pred = (
        (coef[:, None, None] * masked * error).reshape(kinds * PP, count).astype(jnp.bfloat16)
    )
    back_two = row_folder(head_cols, lax.all_gather(grad_pred, "tensor", axis=0, tiled=True))
    head_term = jnp.dot(grad_pred, full_two, preferred_element_type=jnp.float32)
    head_grad = lax.psum_scatter(head_term, "space", scatter_dimension=1, tiled=True)
    grad_two = (back_two * slope(pre_two)).astype(jnp.bfloat16)
    back_one = column_folder(rows_second, lax.all_gather(grad_two, "tensor", axis=1, tiled=True))
    grad_one = (back_one * slope(pre_one)).astype(jnp.bfloat16)
    joined = lax.psum_scatter(
        jnp.concatenate(
            [
                lax.dot_general(
                    full_one, grad_two, (((0,), (0,)), ((), ())), preferred_element_type=jnp.float32
                ),
                lax.dot_general(
                    full_in, grad_one, (((0,), (0,)), ((), ())), preferred_element_type=jnp.float32
                ),
            ],
            axis=1,
        ),
        "space",
        scatter_dimension=0,
        tiled=True,
    )
    second_grad = joined[:, :width]
    first_grad = joined[:, width:]
    token_grad = column_folder(rows_first, lax.all_gather(grad_one, "tensor", axis=1, tiled=True))
    return (loss, token_grad, first_grad, second_grad, head_grad)


def solution(mesh):
    size = mesh.shape["space"]
    paired = mesh.shape["tensor"] == 2 and size == 16
    return jax.shard_map(
        per_device if paired else per_device_wide,
        mesh=mesh,
        in_specs=(
            P("space", "tensor"),
            P(None, "tensor"),
            P(None, "tensor"),
            P("tensor", None),
            P("tensor", "space"),
            P(None, "space"),
            P("tensor"),
            P(),
        ),
        out_specs=(
            P(),
            P("space", "tensor"),
            P("space", "tensor"),
            P("space", "tensor"),
            P("tensor", "space"),
        ),
        check_vma=False,
    )
```

time: 106 us -> 91.3 us (0.86)
  matrix products: 20.5 us -> 0 us
  Pallas kernels: 69.4 us -> 81.3 us
  other arithmetic: 6.32 us -> 3.32 us
  between operations: 3.46 us -> 1.31 us
    dot_general x9 -> x0, matrix products: 20.5 us -> none  [mix(): lax.dot_general(a, b, ((dims[:1], dims[1:]), ((), ())), preferred_element...]
    pallas_call x3 -> x1, Pallas kernels: 69.4 us -> 81.3 us  [fused(): pl.pallas_call(fused_kernel, out_shape=(shape((8, TILE), wide), shape((co...]
    sub x1 -> x0, other arithmetic: 1.6 us -> none  [per_device(): 1.0 - land[None]]
    slice x1, local copies, waits for them, and re-layouts: 0.05 us -> 1.23 us  [per_device(): loss[0, 0]]
    another operation x2 -> x0, other arithmetic: 1.12 us -> none
    convert_element_type x4 -> x2, other arithmetic: 2.45 us -> 3.32 us  [the longest x1 2.66 us: per_device(): token_grad.astype(jnp.float32)]
    unnamed x34 -> x7, local copies, waits for them, and re-layouts: 2.97 us -> 2.92 us
where the time goes in v1:
time: 91.3 us; the launch traced here: 91 us
  Pallas kernels  81.3 us (89%)
  local copies, waits for them, and re-layouts  5.06 us (6%)
  other arithmetic  3.32 us (4%)
  between operations  1.31 us (1%)
    pallas_call x1, Pallas kernels, fused(): pl.pallas_call(fused_kernel, out_shape=(shape((8, TILE), wide), shape((co...  81.3 us
    unnamed x7, local copies, waits for them, and re-layouts  2.92 us
    convert_element_type x1, other arithmetic, per_device(): token_grad.astype(jnp.float32)  2.66 us

profile of v1, /device:TPU:0, one launch (start us, length us, event | category | flops | bytes accessed | tf_op | source)
XLA Modules:
  0.0 91.0 jit_solution(8871149585546986105)
XLA Ops:
  1.3 0.7 convert_element_type.14
  1.9 0.1 broadcast_in_dim.4
  2.0 0.1 convert_element_type.15
  2.1 0.7 broadcast_in_dim.10.label
  2.9 81.3 %fused.1 = (f32[8,128]{1,0:T(8,128)}, bf16[896,512]{1,0:T(8,128)(2,1)}, f32[64,512]{1,0:T(8,128)}, f32[64,512]{1,0:T(8,128)}, f32[176,64]{1,0:T(8,128)}) custom-call(f32[1]{0:T(128)} %bitcast.2.scale, f32[176,128]{1,0:T(8,128)} %broadcast_in_dim.10.label, s32[4,896]{1,0:T(4,128)} %land.1, bf16[896,512]{1,0:T(8,128)(2,1)} %tok.1, bf16[1024,512]{1,0:T(8,128)(2,1)} %one.1, ...), custom_call_target="tpu_custom_call" | custom-call | tf_op jit(solution)/shard_map/fused/pallas_call | solution.py:499
  84.2 0.0 copy-start.1
  84.2 0.0 copy-start
  84.2 1.2 %slice.3 = f32[1,1]{1,0:T(1,128)} slice(f32[8,128]{1,0:T(8,128)} %get-tuple-element.10), slice={[0:1], [0:1]} | slice | bytes 8 | tf_op jit(solution)/shard_map/slice | solution.py:525
  85.5 1.6 %copy.14 = f32[176,64]{0,1:T(8,128)} copy(f32[176,64]{1,0:T(8,128)} %get-tuple-element.24) | data formatting | bytes 90112
  87.1 2.7 %convert_element_type.16 = f32[896,512]{1,0:T(8,128)} convert(bf16[896,512]{1,0:T(8,128)(2,1)} %get-tuple-element.11) | non-fusion elementwise | flops 458752 | bytes 2752512 | tf_op jit(solution)/shard_map/convert_element_type | solution.py:525
  89.7 0.0 copy-done.1
  89.7 0.7 copy.18
  90.4 0.0 copy-done
  90.4 0.7 copy.19
Async XLA Ops:
  84.2 5.5 %copy-start.1 = (f32[64,512]{1,0:T(8,128)S(1)}, f32[64,512]{1,0:T(8,128)}, u32[]{:S(2)}) copy-start(f32[64,512]{1,0:T(8,128)} %get-tuple-element.32) | copy-start | bytes 393220
  84.2 6.2 %copy-start = (f32[64,512]{1,0:T(8,128)S(1)}, f32[64,512]{1,0:T(8,128)}, u32[]{:S(2)}) copy-start(f32[64,512]{1,0:T(8,128)} %get-tuple-element.33) | copy-start | bytes 393220

commit v2 on v1

--- a/solution.py
+++ b/solution.py
@@ -43,24 +43,35 @@
 
 
 TILE = 128
-RELAYS = (
-    (0, 0), (1, 0), (2, 0), (0, 8), (0, 4), (1, 8), (0, 2), (2, 8), (1, 4), (0, 12), (2, 4),
-    (0, 10), (1, 2), (1, 12), (2, 2), (2, 12), (0, 6), (0, 14),
-)
-CORE_SIDE = (1, 9, 5, 13, 3, 11, 7, 15)
-PLAN = ("y", "y", "z", "y", "z")
+TREES = ((2, 1, 0), (3, 2, 1, 0), (1, 3, 2, 0))
+PLAN = (("y", "x", "z"), ("y", "z", "x"), ("z", "y", "x"), ("y", "x", "z"), ("z", "y", "x"))
+BITS = {"z": 2, "y": 1}
+
+
+def stage_shapes(order):
+    found = []
+    lead, lanes = 2, 2 * TILE
+    for way in order[1:]:
+        found.append((2,) * lead + (TILE, lanes))
+        if way == "x":
+            lanes = TILE
+        else:
+            lead -= 1
+    found.append((2,) * lead + (TILE, lanes))
+    return found
 
 
 def fused_kernel(
-    scale, label, land, tok, one, two, head, tar,
+    scale, kinds_in, land, tok, one, two, head, tar,
     o_loss, o_tok, o_one, o_two, o_head,
     w_one, w_two, w_head, toks, tok_out, tar_v, tar_s, tar_all, lnd, masked,
     pre_one, pre_two, h_one, h_two, t_tok, t_one, t_two, tgt, scored, sc_low, sc_par, gp_low,
-    g_two, g_one, p_two, p_one, tg_out, hb,
-    msg, near, far, mid,
-    fars, arrs0, nears0, fars1, arrs1, nears1, fars2, arrs2, nears2, finals, arrs3, arrs4, arrs5,
-    local, wsend, wrecv, xsend, xrecv, dsend, drecv, tsend, trecv, rsend, rrecv,
+    g_two, g_one, p_two, p_one, tg_far, tg_near, r_one, r_two, r_head, hb, r_loss, kb, kp,
+    msg, near, far, mid, finals, arrs3, arrs4, arrs5, *refs,
 ):
+    slices = len(PLAN)
+    fars, arrs, nears = [[refs[j * 3 * slices + g * 3 : j * 3 * slices + g * 3 + 3] for g in range(slices)] for j in range(3)]
+    local, wsend, wrecv, xsend, xrecv, dsend, drecv, tsend, trecv, rsend, rrecv, outs = refs[9 * slices :]
     low, wide = jnp.bfloat16, jnp.float32
     s, x = lax.axis_index("space"), lax.axis_index("tensor")
     other = 1 - x
@@ -75,10 +86,10 @@
     hr = TILE // 2
     across, partner = (s, other), (flipped(s, 0), x)
     diagonal = (flipped(flipped(s, 3), 0), x)
-    started = []
-
-    def at(index, size, base=0):
-        return pl.ds(pl.multiple_of(index * size + base, math.gcd(size, base) if base else size), size)
+    started, writes = [], []
+
+    def at(index, size):
+        return pl.ds(pl.multiple_of(index * size, size), size)
 
     def remote(src, dst, sends, recvs, slot, target):
         copy = pltpu.make_async_remote_copy(
@@ -93,6 +104,11 @@
         started.append(copy)
         return copy
 
+    def write_out(src, dst):
+        copy = pltpu.make_async_copy(src, dst, outs.at[len(writes)])
+        copy.start()
+        writes.append(copy)
+
     moves = [
         (one, w_one.at[:, at(x, width)]),
         (two, w_two.at[:, at(x, width)]),
@@ -113,6 +129,10 @@
     for ref in (toks, h_one, h_two, g_two, g_one, sc_low):
         ref[half:, :] = jnp.zeros((pad - half, ref.shape[1]), low)
     tar_all[:, rows:, :] = jnp.zeros((2, vw - rows, pad), low)
+    kb[...] = jnp.zeros_like(kb)
+    kb[0:1, 0 : rows // PP] = kinds_in[...].astype(wide)
+    lnd[...] = jnp.zeros_like(lnd)
+    lnd[0:PP, :] = land[...].astype(wide)
 
     low_bits, high = s % 4, s // 4
     mine = x * 4 + low_bits
@@ -133,8 +153,10 @@
         for b in range(4):
             if (m >> b) & 1:
                 q = flipped(q, b)
-        if k < 2:
-            return (w_one, w_two)[k].at[at(q, part), at(side, width)]
+        if k == 0:
+            return w_one.at[at(q % 8, 2 * part), at(side, width)]
+        if k == 1:
+            return w_two.at[at(q, part), at(side, width)]
         first = pl.multiple_of(side * vw + (q % 2) * shard, 16)
         return w_head.at[pl.ds(first, shard), at(q // 2, TILE)]
 
@@ -142,6 +164,7 @@
     for k in range(3):
         loads[k].wait()
         pieces[k, 0] = remote(place(k, 0, x), place(k, 0, x), wsend, wrecv, 16 * k, across)
+    kind_copy = remote(kb, kp, xsend, xrecv, 4, across)
     loads[3].wait()
     parts = 2
     step = half // parts
@@ -155,64 +178,58 @@
     ]
     loads[4].wait()
     tail = count - pad
-    spare = lax.broadcasted_iota(jnp.int32, (rows, pad), 1) >= half
-    tags = jnp.concatenate([label[...]] * (pad // TILE), axis=1)
     lo = tar_v[:, :pad]
     hi = pltpu.roll(tar_v[:, tail:], pad - half + tail, 1)
-    tar_s[...] = jnp.where(spare, tags, jnp.where(x == 0, hi, lo)).astype(low)
+    tar_s[...] = jnp.where(x == 0, hi, lo).astype(low)
     tar_copy = remote(tar_s, tar_all.at[x, pl.ds(0, rows), :], xsend, xrecv, parts, across)
-    tar_all[x, 0:rows, :] = jnp.where(spare, tags, jnp.where(x == 0, lo, hi)).astype(low)
+    tar_all[x, 0:rows, :] = jnp.where(x == 0, lo, hi).astype(low)
     loads[5].wait()
 
-    def relay(k, m):
-        pieces[k, m].wait_recv()
-        for b in (3, 2, 1, 0):
-            if m & ((2 << b) - 1) == 0:
+    def relay(k, *ms):
+        for m in ms:
+            pieces[k, m].wait_recv()
+            last = -1
+            for n, b in enumerate(TREES[k]):
+                if (m >> b) & 1:
+                    last = n
+            for b in TREES[k][last + 1 :]:
                 piece = place(k, m, other)
                 new = m ^ (1 << b)
                 pieces[k, new] = remote(piece, piece, wsend, wrecv, 16 * k + new, (flipped(s, b), x))
 
-    for k, m in RELAYS:
-        relay(k, m)
-    for m in CORE_SIDE:
-        relay(0, m)
-
-    def one_rows(first, size):
+    def layer(src, first, size, weight, side, pre, dst):
+        span = slice(first, first + size)
+        for i in range(width // vw):
+            tile = pl.ds(pl.multiple_of(side * width + i * vw, vw), vw)
+            z = jnp.dot(src[span, :], weight[:, tile], preferred_element_type=wide)
+            pre[span, tile] = z
+            dst[span, tile] = bent(z)
+
+    def flip_to(src, dst, slot):
+        for n in range(dim // TILE):
+            dst[0, n * TILE : (n + 1) * TILE, :] = src[:, n * TILE : (n + 1) * TILE].T
+        return remote(dst.at[0], dst.at[1], dsend, drecv, slot, partner)
+
+    def make_slope(ref):
         def body(n, _):
-            z = jnp.dot(toks[first : first + size, :], w_one[:, at(n, vw)], preferred_element_type=wide)
-            pre_one[first : first + size, at(n, vw)] = z
-            h_one[first : first + size, at(n, vw)] = bent(z)
+            ref[:, at(n, TILE)] = slope(ref[:, at(n, TILE)])
             return 0
 
-        lax.fori_loop(0, dim // vw, body, 0)
-
-    for n in range(parts):
-        tok_copies[n].wait_recv()
-        one_rows(n * step, step)
-    for k, m in ((1, 10), (2, 10), (1, 6), (1, 14), (2, 6), (2, 14)):
-        relay(k, m)
-    for m in CORE_SIDE:
-        relay(1, m)
-
-    def two_body(n, _):
-        z = jnp.dot(h_one[0:half, :], w_two[:, at(n, vw)], preferred_element_type=wide)
-        pre_two[:, at(n, vw)] = z
-        h_two[0:half, at(n, vw)] = bent(z)
-        return 0
-
-    lax.fori_loop(0, dim // vw, two_body, 0)
-    for m in CORE_SIDE:
-        relay(2, m)
-    tar_copy.wait_recv()
-
-    for side in range(2):
-        tgt[:, side * vw : (side + 1) * vw] = tar_all[side].astype(wide).T
+        lax.fori_loop(0, dim // TILE, body, 0)
+
+    relay(0, 0)
+    relay(1, 0)
+    relay(2, 0)
+    kind_copy.wait_recv()
     lane = lax.broadcasted_iota(jnp.int32, (1, 2 * vw), 1)
     used = lane % vw < rows
-    kind = tgt[half : half + 1, :]
     cell = lane % PP
-    lnd[...] = jnp.zeros_like(lnd)
-    lnd[0:PP, :] = land[...].astype(wide)
+    group_shape = (TILE, vw)
+    group = lax.broadcasted_iota(jnp.int32, group_shape, 1) // PP == lax.broadcasted_iota(jnp.int32, group_shape, 0)
+    group = jnp.where(group, 1.0, 0.0).astype(low)
+    k_own = jnp.dot(kb[...].astype(low), group, preferred_element_type=wide)[0:1, :]
+    k_oth = jnp.dot(kp[...].astype(low), group, preferred_element_type=wide)[0:1, :]
+    kind = jnp.concatenate([jnp.where(x == 0, k_own, k_oth), jnp.where(x == 0, k_oth, k_own)], axis=1)
     ground = jnp.where(x == 0, lnd[:, :pad], pltpu.roll(lnd[:, tail:], pad - half + tail, 1))
     pick_shape = (TILE, 2 * vw)
     pick = lax.broadcasted_iota(jnp.int32, pick_shape, 1) % PP == lax.broadcasted_iota(jnp.int32, pick_shape, 0)
@@ -229,7 +246,32 @@
         slant = jnp.where(kind == 1.0, weight, jnp.where(kind == 2.0, -weight, 0.0))
         band = slice(j * LONP, (j + 1) * LONP)
         masked[band, :] = flat + slant * spread[band, :]
-
+    relay(0, 4, 2)
+    relay(1, 2, 4)
+    relay(2, 2)
+    relay(1, 8)
+    tgt[:, at(x, vw)] = tar_all[x].astype(wide).T
+    relay(2, 4, 8)
+    tok_copies[0].wait_recv()
+    layer(toks, 0, step, w_one, x, pre_one, h_one)
+    relay(0, 6)
+    relay(1, 12)
+    relay(2, 6)
+    relay(0, 1, 5, 3, 7)
+    layer(toks, 0, step, w_one, other, pre_one, h_one)
+    relay(1, 6)
+    relay(2, 10, 12, 14)
+    tok_copies[1].wait_recv()
+    layer(toks, step, half - step, w_one, x, pre_one, h_one)
+    layer(toks, step, half - step, w_one, other, pre_one, h_one)
+    relay(1, 10, 14)
+    layer(h_one, 0, half, w_two, x, pre_two, h_two)
+    flips = [flip_to(toks, t_tok, 4)]
+    relay(1, 1, 9, 5, 13, 3, 11, 7, 15)
+    layer(h_one, 0, half, w_two, other, pre_two, h_two)
+    relay(2, 1, 9, 5, 13, 3, 11, 7, 15)
+    tar_copy.wait_recv()
+    tgt[:, at(other, vw)] = tar_all[other].astype(wide).T
     for side in range(2):
         cols = slice(side * vw, (side + 1) * vw)
         error = lax.dot_general(
@@ -261,86 +303,71 @@
         remote(sc_low.at[:, scored_cols(n, oc)], sc_par.at[:, pl.ds(n * TILE, TILE)], dsend, drecv, n, partner)
         for n in range(2)
     ]
-
-    def flip_to(src, dst, slot):
-        def body(n, _):
-            dst[0, at(n, TILE), :] = src[:, at(n, TILE)].T
-            return 0
-
-        lax.fori_loop(0, dim // TILE, body, 0)
-        return remote(dst.at[0], dst.at[1], dsend, drecv, slot, partner)
-
-    flips = [flip_to(h_two, t_two, 2)]
+    flips = [flip_to(h_two, t_two, 2), flip_to(h_one, t_one, 3)] + flips
+    make_slope(pre_two)
     for copy in first_share:
         copy.wait_recv()
     mid[...] = jnp.sum(near[...], axis=0)
     second_share = share(mid, far, high, [far_peer(d) for d in range(1, 4)], 7)
-    flips += [flip_to(h_one, t_one, 3), flip_to(toks, t_tok, 4)]
-
-    def make_slope(ref):
-        def body(n, _):
-            ref[:, at(n, TILE)] = slope(ref[:, at(n, TILE)])
-            return 0
-
-        lax.fori_loop(0, dim // TILE, body, 0)
-
-    ways = {"z": (zn, 2), "y": (yy, 1)}
+
+    mark_bits = {"z": zn, "y": yy}
 
     def produce(g, trans, own_cols, par_cols):
-        value, bit = ways[PLAN[g]]
+        first = PLAN[g][0]
+        value = mark_bits[first]
+        both_cols = jnp.concatenate([own_cols, par_cols], axis=0)
 
         def product(v):
             def side_rows(k):
                 blocks = []
                 for i in range(2):
                     for j in range(2):
-                        index = i * 4 + (j * 2 + v if PLAN[g] == "y" else v * 2 + j)
+                        index = i * 4 + (j * 2 + v if first == "y" else v * 2 + j)
                         blocks.append(trans[k, at(index, TILE), :])
                 return jnp.concatenate(blocks, axis=0)
 
-            out = jnp.dot(side_rows(0), own_cols, preferred_element_type=wide)
-            out += jnp.dot(side_rows(1), par_cols, preferred_element_type=wide)
+            both_rows = jnp.concatenate([side_rows(0), side_rows(1)], axis=1)
+            out = jnp.dot(both_rows, both_cols, preferred_element_type=wide)
             return out.reshape(2, 2, TILE, vw)
 
-        fars[g] = product(1 - value).astype(low)
-        copy = remote(fars.at[g], arrs0.at[g], rsend, rrecv, 6 * g, (flipped(s, bit), x))
-        nears0[g] = product(value)
+        fars[g][0][...] = product(1 - value).astype(low)
+        copy = remote(fars[g][0], arrs[g][0], rsend, rrecv, 6 * g, (flipped(s, BITS[first]), x))
+        nears[g][0][...] = product(value)
         return copy
 
-    def advance_one(g, copy):
+    def advance(g, n, copy):
         copy.wait_recv()
-        value, bit = ways["z" if PLAN[g] == "y" else "y"]
-        fars1[g] = (nears0[g, :, 1 - value] + arrs0[g, :, 1 - value].astype(wide)).astype(low)
-        copy = remote(fars1.at[g], arrs1.at[g], rsend, rrecv, 6 * g + 1, (flipped(s, bit), x))
-        nears1[g] = nears0[g, :, value] + arrs0[g, :, value].astype(wide)
+        way = PLAN[g][n]
+        ref, came = nears[g][n - 1], arrs[g][n - 1]
+        if way == "x":
+            lead = (slice(None),) * (len(ref.shape) - 1)
+            away, here, target = lead + (at(other, TILE),), lead + (at(x, TILE),), across
+        else:
+            value = mark_bits[way]
+            away, here = (slice(None), 1 - value), (slice(None), value)
+            target = (flipped(s, BITS[way]), x)
+        fars[g][n][...] = (ref[away] + came[away].astype(wide)).astype(low)
+        copy = remote(fars[g][n], arrs[g][n], rsend, rrecv, 6 * g + n, target)
+        nears[g][n][...] = ref[here] + came[here].astype(wide)
         return copy
 
-    def advance_two(g, copy):
+    def advance_last(g, copy):
         copy.wait_recv()
-        away, here = at(other, TILE), at(x, TILE)
-        fars2[g] = (nears1[g, :, :, away] + arrs1[g, :, :, away].astype(wide)).astype(low)
-        copy = remote(fars2.at[g], arrs2.at[g], rsend, rrecv, 6 * g + 2, across)
-        nears2[g] = nears1[g, :, :, here] + arrs1[g, :, :, here].astype(wide)
-        return copy
-
-    def advance_three(g, copy):
-        copy.wait_recv()
-        finals[g] = (nears2[g, 1 - zf] + arrs2[g, 1 - zf].astype(wide)).astype(low)
+        ref, came = nears[g][2], arrs[g][2]
+        finals[g] = (ref[1 - zf] + came[1 - zf].astype(wide)).astype(low)
         up = (flipped(s, 3), x)
         copies = [
             remote(finals.at[g, at(core, hr), :], arrs4.at[g], rsend, rrecv, 6 * g + 3, up),
             remote(finals.at[g, at(oc, hr), :], arrs5.at[g], rsend, rrecv, 6 * g + 4, diagonal),
         ]
-        nears2[g, zf] = nears2[g, zf] + arrs2[g, zf].astype(wide)
-        copies.append(
-            remote(nears2.at[g, zf, at(oc, hr), :], arrs3.at[g], rsend, rrecv, 6 * g + 5, partner)
-        )
+        ref[zf] = ref[zf] + came[zf].astype(wide)
+        copies.append(remote(ref.at[zf, at(oc, hr), :], arrs3.at[g], rsend, rrecv, 6 * g + 5, partner))
         return copies
 
     def finish(g, copies, out, base):
         for copy in copies:
             copy.wait_recv()
-        kept = nears2[g, zf, at(core, hr), :] + arrs4[g].astype(wide)
+        kept = nears[g][2][zf, at(core, hr), :] + arrs4[g].astype(wide)
         came = arrs3[g] + arrs5[g].astype(wide)
         span = out.shape[1] // 2
         out[pl.ds(0, hr), pl.ds(pl.multiple_of(core * span + base, TILE), TILE)] = kept
@@ -352,8 +379,7 @@
     state = {}
     own = jnp.concatenate([sc_low[:, scored_cols(n, core)] for n in range(2)], axis=1)
     state[0] = produce(0, t_two, own, sc_par[...])
-    make_slope(pre_two)
-
+    make_slope(pre_one)
     for copy in second_share:
         copy.wait_recv()
     sums = jnp.sum(far[...], axis=0)
@@ -368,32 +394,30 @@
     root = jnp.sqrt(jnp.where(ok, sums[0:4, :], 0.0) / weight_sum + 1e-06)
     roots = jnp.where(ok & (tl % PP == 0), root, 0.0)
     loss = jnp.sum(jnp.sum(roots, axis=0, keepdims=True), axis=1, keepdims=True) / kinds
-    o_loss[...] = jnp.broadcast_to(loss, o_loss.shape)
+    r_loss[...] = jnp.broadcast_to(loss, r_loss.shape)
+    write_out(r_loss, o_loss)
     coef = jnp.where(ok, scale[0] / (kinds * root * weight_sum), 0.0)
     coef = jnp.concatenate([coef[n : n + 1, :] for n in range(4)], axis=1)
     gp_low[...] = (coef * scored[...]).astype(low)
 
     def grad_tiles(made, send_to, base, make):
-        copies = []
-        for c in (oc, core):
-            for side in range(2):
-                tile = pl.ds(pl.multiple_of(side * width + c * vw, vw), vw)
-                made[0:half, tile] = make(tile)
-                if c is oc:
-                    copies.append(
-                        remote(
-                            made.at[:, tile], send_to.at[:, pl.ds(side * vw, vw)],
-                            dsend, drecv, base + side, partner,
-                        )
-                    )
-        return copies
+        for n in range(dim // vw):
+            tile = pl.ds(n * vw, vw)
+            made[0:half, tile] = make(tile)
+        return [
+            remote(
+                made.at[:, pl.ds(pl.multiple_of(side * width + oc * vw, vw), vw)],
+                send_to.at[:, pl.ds(side * vw, vw)],
+                dsend, drecv, base + side, partner,
+            )
+            for side in range(2)
+        ]
 
     def make_two(tile):
         b = jnp.dot(gp_low[...], w_head[:, tile], preferred_element_type=wide)
         return (b * pre_two[:, tile]).astype(low)
 
     two_copies = grad_tiles(g_two, p_two, 5, make_two)
-    make_slope(pre_one)
 
     def make_one(tile):
         b = lax.dot_general(
@@ -410,18 +434,7 @@
         par_cols = [came[:, n * vw + a * TILE : n * vw + (a + 1) * TILE] for n in range(2)]
         return jnp.concatenate(own_cols, axis=1), jnp.concatenate(par_cols, axis=1)
 
-    for copy in two_copies + [flips[1]]:
-        copy.wait_recv()
-    for a in range(2):
-        state[1 + a] = produce(1 + a, t_one, *both(g_two, p_two, a))
-    state[0] = advance_one(0, state[0])
-    for copy in one_copies + [flips[2]]:
-        copy.wait_recv()
-    for a in range(2):
-        state[3 + a] = produce(3 + a, t_tok, *both(g_one, p_one, a))
-    state[0] = advance_two(0, state[0])
-
-    def token_side(side, write):
+    def token_side(side, out):
         for n in range(width // vw):
             b = lax.dot_general(
                 g_one[0:half, :],
@@ -429,48 +442,58 @@
                 (((1,), (1,)), ((), ())),
                 preferred_element_type=wide,
             )
-            write(n, b.astype(low))
-
-    def write_far(n, b):
-        tg_out[:, n * vw : (n + 1) * vw] = b
-
-    def write_near(n, b):
-        o_tok[at(x, half), n * vw : (n + 1) * vw] = b
-
-    token_side(other, write_far)
-    tg_copy = remote(tg_out, o_tok.at[at(x, half), :], xsend, xrecv, parts + 1, across)
-    state[1] = advance_one(1, state[1])
-    state[2] = advance_one(2, state[2])
-    token_side(x, write_near)
-    state[0] = advance_three(0, state[0])
-    state[3] = advance_one(3, state[3])
-    state[1] = advance_two(1, state[1])
-    state[2] = advance_two(2, state[2])
-    state[4] = advance_one(4, state[4])
+            out[:, n * vw : (n + 1) * vw] = b.astype(low)
+
+    for copy in two_copies + [flips[1]]:
+        copy.wait_recv()
+    for a in range(2):
+        state[1 + a] = produce(1 + a, t_one, *both(g_two, p_two, a))
+    token_side(other, tg_far)
+    state[0] = advance(0, 1, state[0])
+    tg_copy = remote(tg_far, o_tok.at[at(x, half), :], xsend, xrecv, parts + 1, across)
+    for copy in one_copies + [flips[2]]:
+        copy.wait_recv()
+    for a in range(2):
+        state[3 + a] = produce(3 + a, t_tok, *both(g_one, p_one, a))
+    token_side(x, tg_near)
+    write_out(tg_near, o_tok.at[at(x, half), :])
+    state[0] = advance(0, 2, state[0])
+    state[1] = advance(1, 1, state[1])
+    state[2] = advance(2, 1, state[2])
+    state[3] = advance(3, 1, state[3])
+    state[4] = advance(4, 1, state[4])
+    state[0] = advance_last(0, state[0])
+    state[2] = advance(2, 2, state[2])
+    state[1] = advance(1, 2, state[1])
+    state[3] = advance(3, 2, state[3])
+    state[4] = advance(4, 2, state[4])
     finish(0, state[0], hb, 0)
     coef_here = jnp.where(x == 0, coef[:, :vw], coef[:, vw:])
-    o_head[...] = (hb[...] * coef_here).T[0:rows, 0:hr]
-    state[1] = advance_three(1, state[1])
-    state[2] = advance_three(2, state[2])
-    state[3] = advance_two(3, state[3])
-    state[4] = advance_two(4, state[4])
-    finish(1, state[1], o_two, 0)
-    finish(2, state[2], o_two, TILE)
-    state[3] = advance_three(3, state[3])
-    state[4] = advance_three(4, state[4])
-    finish(3, state[3], o_one, 0)
-    finish(4, state[4], o_one, TILE)
+    r_head[...] = (hb[...] * coef_here)[:, 0:rows]
+    write_out(r_head, o_head)
+    state[2] = advance_last(2, state[2])
+    state[1] = advance_last(1, state[1])
+    state[3] = advance_last(3, state[3])
+    state[4] = advance_last(4, state[4])
+    finish(2, state[2], r_two, TILE)
+    finish(1, state[1], r_two, 0)
+    write_out(r_two, o_two)
+    finish(3, state[3], r_one, 0)
+    finish(4, state[4], r_one, TILE)
+    write_out(r_one, o_one)
     tg_copy.wait_recv()
     for copy in started:
         copy.wait_send()
-
-
-def fused(scale, label, land, tokens, first, second, head, targets):
+    for copy in writes:
+        copy.wait()
+
+
+def fused(scale, kinds, land, tokens, first, second, head, targets):
     count, width = tokens.shape
     dim = first.shape[0]
     rows = head.shape[0]
     half = count // 2
-    pad = -(-(half + 1) // TILE) * TILE
+    pad = -(-half // TILE) * TILE
     vw = 2 * TILE
     hr = TILE // 2
     low, wide = jnp.bfloat16, jnp.float32
@@ -486,15 +509,17 @@
         vm((pad, 2 * vw), wide), vm((half, 2 * vw), wide), vm((pad, 2 * vw), low), vm((pad, vw), low),
         vm((half, 2 * vw), low),
         vm((pad, dim), low), vm((pad, dim), low), vm((pad, width), low), vm((pad, width), low),
-        vm((half, width), low), vm((TILE, vw), wide),
+        vm((half, width), low), vm((half, width), low),
+        vm((hr, width), wide), vm((hr, width), wide), vm((hr, rows), wide), vm((hr, vw), wide),
+        vm((8, TILE), wide), vm((8, TILE), wide), vm((8, TILE), wide),
         vm((8, TILE), wide), vm((8, 8, TILE), wide), vm((4, 8, TILE), wide), vm((8, TILE), wide),
-        vm((slices, 2, 2, TILE, vw), low), vm((slices, 2, 2, TILE, vw), low), vm((slices, 2, 2, TILE, vw), wide),
-        vm((slices, 2, TILE, vw), low), vm((slices, 2, TILE, vw), low), vm((slices, 2, TILE, vw), wide),
-        vm((slices, 2, TILE, TILE), low), vm((slices, 2, TILE, TILE), low), vm((slices, 2, TILE, TILE), wide),
         vm((slices, TILE, TILE), low), vm((slices, hr, TILE), wide),
         vm((slices, hr, TILE), low), vm((slices, hr, TILE), low),
     ]
-    sizes = (6, 48, 48, 4, 4, 9, 9, 10, 10, 6 * slices, 6 * slices)
+    for kind in (low, low, wide):
+        for order in PLAN:
+            scratch += [vm(found, kind) for found in stage_shapes(order)]
+    sizes = (6, 48, 48, 5, 5, 9, 9, 10, 10, 6 * slices, 6 * slices, 5)
     scratch += [pltpu.SemaphoreType.DMA((n,)) for n in sizes]
     return pl.pallas_call(
         fused_kernel,
@@ -503,26 +528,79 @@
             shape((count, width), low),
             shape((dim // 16, width), wide),
             shape((dim // 16, width), wide),
-            shape((rows, hr), wide),
+            shape((hr, rows), wide),
         ),
         in_specs=[pl.BlockSpec(memory_space=pltpu.SMEM), VMEM, VMEM] + [ANY] * 5,
-        out_specs=[VMEM] * 5,
+        out_specs=[ANY] * 5,
         scratch_shapes=scratch,
         compiler_params=params(0, 56),
         name="fused",
-    )(scale, label, land, tokens, first, second, head, targets)
+    )(scale, kinds, land, tokens, first, second, head, targets)
+
+
+CHUNKS = 4
+
+
+def write_kernel(
+    loss, tok, one, two, head, o_loss, o_tok, o_one, o_two, o_head,
+    v_loss, v_tok, v_one, v_two, v_head, f_loss, f_tok, came, went,
+):
+    size = tok.shape[0] // CHUNKS
+    loads = [
+        pltpu.make_async_copy(tok.at[pl.ds(n * size, size), :], v_tok.at[pl.ds(n * size, size), :], came.at[n])
+        for n in range(CHUNKS)
+    ]
+    small = [(one, v_one, o_one), (two, v_two, o_two), (head, v_head, o_head), (loss, v_loss, None)]
+    loads += [pltpu.make_async_copy(a, b, came.at[CHUNKS + n]) for n, (a, b, _) in enumerate(small)]
+    for copy in loads:
+        copy.start()
+    stores = []
+
+    def store(src, dst):
+        copy = pltpu.make_async_copy(src, dst, went.at[len(stores)])
+        copy.start()
+        stores.append(copy)
+
+    for n in range(CHUNKS):
+        loads[n].wait()
+        span = pl.ds(n * size, size)
+        f_tok[span, :] = v_tok[span, :].astype(jnp.float32)
+        store(f_tok.at[span, :], o_tok.at[span, :])
+    for n, (_, b, c) in enumerate(small):
+        loads[CHUNKS + n].wait()
+        if c is None:
+            f_loss[...] = b[0:1, 0:1]
+            b, c = f_loss, o_loss
+        store(b, c)
+    for copy in stores:
+        copy.wait()
+
+
+def write(*parts):
+    wide = jnp.float32
+    shapes = [(1, 1)] + [p.shape for p in parts[1:]]
+    vm = pltpu.VMEM
+    return pl.pallas_call(
+        write_kernel,
+        out_shape=tuple(jax.ShapeDtypeStruct(a, wide) for a in shapes),
+        in_specs=[ANY] * 5,
+        out_specs=[ANY] * 5,
+        scratch_shapes=[vm(p.shape, p.dtype) for p in parts]
+        + [vm((1, 1), wide), vm(parts[1].shape, wide)]
+        + [pltpu.SemaphoreType.DMA((CHUNKS + 4,)), pltpu.SemaphoreType.DMA((CHUNKS + 4,))],
+        name="write",
+    )(*parts)
 
 
 def per_device(
     tokens, first_weight, second_weight, head_weight, targets, land_mask, variable_kind, loss_scale
 ):
-    rows = head_weight.shape[0]
-    label = jnp.repeat(variable_kind, PP).astype(jnp.float32)[:, None]
-    label = jnp.broadcast_to(label, (rows, TILE))
-    loss, token_grad, first_grad, second_grad, head_grad = fused(
-        loss_scale.reshape(1), label, land_mask, tokens, first_weight, second_weight, head_weight, targets
-    )
-    return (loss[0, 0], token_grad.astype(jnp.float32), first_grad, second_grad, head_grad)
+    parts = fused(
+        loss_scale.reshape(1), variable_kind.reshape(1, -1), land_mask,
+        tokens, first_weight, second_weight, head_weight, targets,
+    )
+    loss, token_grad, first_grad, second_grad, head_grad = write(*parts)
+    return (loss.reshape(()), token_grad, first_grad, second_grad, head_grad.T)
 
 
 def column_folder(weights, piece):

time: 91.3 us -> 75.1 us (0.82)
  Pallas kernels: 81.3 us -> 73.4 us
  local copies, waits for them, and re-layouts: 5.06 us -> 0 us
  other arithmetic: 3.32 us -> 0 us
    pallas_call x1, Pallas kernels: 81.3 us -> 71 us  [fused(): pl.pallas_call(fused_kernel, out_shape=(shape((8, TILE), wide), shape((co...]
    convert_element_type x2 -> x0, other arithmetic: 3.32 us -> none  [the longest x1 2.66 us: per_device(): token_grad.astype(jnp.float32)]
    unnamed x7 -> x0, local copies, waits for them, and re-layouts: 2.92 us -> none
    pallas_call x0 -> x1, Pallas kernels: none -> 2.43 us  [write(): pl.pallas_call(write_kernel, out_shape=tuple((jax.ShapeDtypeStruct(a, wid...]
    slice x1 -> x0, local copies, waits for them, and re-layouts: 1.23 us -> none  [per_device(): loss[0, 0]]
where the time goes in v2:
time: 75.1 us; the launch traced here: 74.8 us
  Pallas kernels  73.4 us (98%)
  between operations  1.45 us (2%)
    pallas_call x1, Pallas kernels, fused(): pl.pallas_call(fused_kernel, out_shape=(shape((8, TILE), wide), shape((co...  71 us
    pallas_call x1, Pallas kernels, write(): pl.pallas_call(write_kernel, out_shape=tuple((jax.ShapeDtypeStruct(a, wid...  2.43 us

profile of v2, /device:TPU:0, one launch (start us, length us, event | category | flops | bytes accessed | tf_op | source)
XLA Modules:
  0.0 74.8 jit_solution(10587762924164304900)
XLA Ops:
  1.3 71.0 %fused.1 = (f32[8,128]{1,0:T(8,128)}, bf16[896,512]{1,0:T(8,128)(2,1)}, f32[64,512]{1,0:T(8,128)}, f32[64,512]{1,0:T(8,128)}, f32[64,176]{1,0:T(8,128)}) custom-call(f32[1]{0:T(128)} %bitcast.4.scale, s32[1,44]{1,0:T(1,128)} %bitcast.5, s32[4,896]{1,0:T(4,128)} %land.1, bf16[896,512]{1,0:T(8,128)(2,1)} %tok.1, bf16[1024,512]{1,0:T(8,128)(2,1)} %one.1, ...), custom_call_target="tpu_custom_call" | custom-call | tf_op jit(solution)/shard_map/fused/pallas_call | solution.py:524
  72.2 2.4 %write.1 = (f32[1,1]{1,0:T(1,128)}, f32[896,512]{1,0:T(8,128)}, f32[64,512]{1,0:T(8,128)}, f32[64,512]{1,0:T(8,128)}, f32[64,176]{1,0:T(8,128)}) custom-call(f32[8,128]{1,0:T(8,128)} %get-tuple-element.15.loss, bf16[896,512]{1,0:T(8,128)(2,1)} %get-tuple-element.16.tok, f32[64,512]{1,0:T(8,128)} %get-tuple-element.17.one, f32[64,512]{1,0:T(8,128)} %get-tuple-element.18.two, ...), custom_call_target="tpu_custom_call" | custom-call | tf_op jit(solution)/shard_map/write/pallas_call | solution.py:583

commit v3 on v2

--- a/solution.py
+++ b/solution.py
@@ -42,22 +42,31 @@
     )
 
 
+HBM = pl.BlockSpec(memory_space=pltpu.HBM)
 TILE = 128
 TREES = ((2, 1, 0), (3, 2, 1, 0), (1, 3, 2, 0))
-PLAN = (("y", "x", "z"), ("y", "z", "x"), ("z", "y", "x"), ("y", "x", "z"), ("z", "y", "x"))
+SLICES = 5
 BITS = {"z": 2, "y": 1}
+PLAN = {
+    (0, 0): "yzx", (0, 1): "yxz", (1, 0): "zyx", (1, 1): "yxz", (2, 0): "yzx", (2, 1): "zyx", (3, 0): "zyx",
+    (3, 1): "yxz", (4, 0): "zxy", (4, 1): "yzx",
+}
+STEPS = (
+    "C", "A001", "T1", "P20", "P21", "T0", "P40", "P41", "A011", "P10", "P11", "A002", "P31", "N", "P30",
+    "A201", "A211", "A411", "A401", "A111", "A101", "A012", "A311", "A301", "A402", "A212", "A202", "A112",
+    "A102", "A412", "A312", "L0", "A302", "L2", "L1", "L4", "L3", "F0", "F2", "F1", "F4", "F3",
+)
 
 
 def stage_shapes(order):
     found = []
-    lead, lanes = 2, 2 * TILE
-    for way in order[1:]:
-        found.append((2,) * lead + (TILE, lanes))
+    left, lanes = 3, 2 * TILE
+    for way in order:
         if way == "x":
             lanes = TILE
         else:
-            lead -= 1
-    found.append((2,) * lead + (TILE, lanes))
+            left -= 1
+        found.append((2,) * left + (TILE // 2, lanes))
     return found
 
 
@@ -66,12 +75,17 @@
     o_loss, o_tok, o_one, o_two, o_head,
     w_one, w_two, w_head, toks, tok_out, tar_v, tar_s, tar_all, lnd, masked,
     pre_one, pre_two, h_one, h_two, t_tok, t_one, t_two, tgt, scored, sc_low, sc_par, gp_low,
-    g_two, g_one, p_two, p_one, tg_far, tg_near, r_one, r_two, r_head, hb, r_loss, kb, kp,
+    g_two, g_one, p_two, p_one, tg_far, hb, kb, kp,
     msg, near, far, mid, finals, arrs3, arrs4, arrs5, *refs,
 ):
-    slices = len(PLAN)
-    fars, arrs, nears = [[refs[j * 3 * slices + g * 3 : j * 3 * slices + g * 3 + 3] for g in range(slices)] for j in range(3)]
-    local, wsend, wrecv, xsend, xrecv, dsend, drecv, tsend, trecv, rsend, rrecv, outs = refs[9 * slices :]
+    keys = sorted(PLAN)
+    pick_refs = iter(refs)
+    fars, arrs, nears = [{key: [next(pick_refs), next(pick_refs)] for key in keys} for _ in range(3)]
+    fars2, arrs2, nears2 = [next(pick_refs) for _ in range(3)]
+    for store, final in ((fars, fars2), (arrs, arrs2), (nears, nears2)):
+        for g, h in keys:
+            store[g, h].append(final.at[g, h])
+    local, wsend, wrecv, xsend, xrecv, dsend, drecv, tsend, trecv, rsend, rrecv = pick_refs
     low, wide = jnp.bfloat16, jnp.float32
     s, x = lax.axis_index("space"), lax.axis_index("tensor")
     other = 1 - x
@@ -86,7 +100,7 @@
     hr = TILE // 2
     across, partner = (s, other), (flipped(s, 0), x)
     diagonal = (flipped(flipped(s, 3), 0), x)
-    started, writes = [], []
+    started = []
 
     def at(index, size):
         return pl.ds(pl.multiple_of(index * size, size), size)
@@ -103,11 +117,6 @@
         copy.start()
         started.append(copy)
         return copy
-
-    def write_out(src, dst):
-        copy = pltpu.make_async_copy(src, dst, outs.at[len(writes)])
-        copy.start()
-        writes.append(copy)
 
     moves = [
         (one, w_one.at[:, at(x, width)]),
@@ -260,13 +269,13 @@
     relay(0, 1, 5, 3, 7)
     layer(toks, 0, step, w_one, other, pre_one, h_one)
     relay(1, 6)
-    relay(2, 10, 12, 14)
+    relay(2, 10, 12)
     tok_copies[1].wait_recv()
     layer(toks, step, half - step, w_one, x, pre_one, h_one)
     layer(toks, step, half - step, w_one, other, pre_one, h_one)
     relay(1, 10, 14)
     layer(h_one, 0, half, w_two, x, pre_two, h_two)
-    flips = [flip_to(toks, t_tok, 4)]
+    relay(2, 14)
     relay(1, 1, 9, 5, 13, 3, 11, 7, 15)
     layer(h_one, 0, half, w_two, other, pre_two, h_two)
     relay(2, 1, 9, 5, 13, 3, 11, 7, 15)
@@ -303,7 +312,7 @@
         remote(sc_low.at[:, scored_cols(n, oc)], sc_par.at[:, pl.ds(n * TILE, TILE)], dsend, drecv, n, partner)
         for n in range(2)
     ]
-    flips = [flip_to(h_two, t_two, 2), flip_to(h_one, t_one, 3)] + flips
+    flips = [flip_to(h_two, t_two, 2), flip_to(h_one, t_one, 3), flip_to(toks, t_tok, 4)]
     make_slope(pre_two)
     for copy in first_share:
         copy.wait_recv()
@@ -312,62 +321,74 @@
 
     mark_bits = {"z": zn, "y": yy}
 
-    def produce(g, trans, own_cols, par_cols):
-        first = PLAN[g][0]
-        value = mark_bits[first]
+    def goal(way):
+        return across if way == "x" else (flipped(s, BITS[way]), x)
+
+    def produce(g, h, trans, own_cols, par_cols):
+        first = PLAN[g, h][0]
         both_cols = jnp.concatenate([own_cols, par_cols], axis=0)
-
-        def product(v):
-            def side_rows(k):
-                blocks = []
-                for i in range(2):
-                    for j in range(2):
-                        index = i * 4 + (j * 2 + v if first == "y" else v * 2 + j)
-                        blocks.append(trans[k, at(index, TILE), :])
-                return jnp.concatenate(blocks, axis=0)
-
-            both_rows = jnp.concatenate([side_rows(0), side_rows(1)], axis=1)
-            out = jnp.dot(both_rows, both_cols, preferred_element_type=wide)
-            return out.reshape(2, 2, TILE, vw)
-
-        fars[g][0][...] = product(1 - value).astype(low)
-        copy = remote(fars[g][0], arrs[g][0], rsend, rrecv, 6 * g, (flipped(s, BITS[first]), x))
-        nears[g][0][...] = product(value)
+        ref, store = fars[g, h][0], nears[g, h][0]
+
+        def product(blocks):
+            sides = [
+                jnp.concatenate(
+                    [trans[k, pl.ds(pl.multiple_of(b * TILE + h * hr, hr), hr), :] for b in blocks], axis=0
+                )
+                for k in range(2)
+            ]
+            return jnp.dot(jnp.concatenate(sides, axis=1), both_cols, preferred_element_type=wide)
+
+        def blocks_of(v):
+            return [i * 4 + (j * 2 + v if first == "y" else v * 2 + j) for i in range(2) for j in range(2)]
+
+        if first == "x":
+            out = product(list(range(8)))
+            ref[...] = jnp.where(x == 0, out[:, TILE:], out[:, :TILE]).astype(low).reshape(ref.shape)
+            store[...] = jnp.where(x == 0, out[:, :TILE], out[:, TILE:]).reshape(ref.shape)
+        else:
+            value = mark_bits[first]
+            out = product(blocks_of(1 - value) + blocks_of(value))
+            ref[...] = out[: 4 * hr].astype(low).reshape(ref.shape)
+        copy = remote(ref, arrs[g, h][0], rsend, rrecv, 9 * g + 3 * h, goal(first))
+        if first != "x":
+            store[...] = out[4 * hr :].reshape(ref.shape)
         return copy
 
-    def advance(g, n, copy):
+    def advance(g, h, n, copy):
         copy.wait_recv()
-        way = PLAN[g][n]
-        ref, came = nears[g][n - 1], arrs[g][n - 1]
+        order = PLAN[g, h]
+        way = order[n]
+        left = [d for d in "fzy" if d not in order[:n]]
+        ref, came = nears[g, h][n - 1], arrs[g, h][n - 1]
         if way == "x":
-            lead = (slice(None),) * (len(ref.shape) - 1)
-            away, here, target = lead + (at(other, TILE),), lead + (at(x, TILE),), across
+            lead = (slice(None),) * (len(left) + 1)
+            away, here = lead + (at(other, TILE),), lead + (at(x, TILE),)
         else:
-            value = mark_bits[way]
-            away, here = (slice(None), 1 - value), (slice(None), value)
-            target = (flipped(s, BITS[way]), x)
-        fars[g][n][...] = (ref[away] + came[away].astype(wide)).astype(low)
-        copy = remote(fars[g][n], arrs[g][n], rsend, rrecv, 6 * g + n, target)
-        nears[g][n][...] = ref[here] + came[here].astype(wide)
+            lead = (slice(None),) * left.index(way)
+            away, here = lead + (1 - mark_bits[way],), lead + (mark_bits[way],)
+        fars[g, h][n][...] = (ref[away] + came[away].astype(wide)).astype(low)
+        copy = remote(fars[g, h][n], arrs[g, h][n], rsend, rrecv, 9 * g + 3 * h + n, goal(way))
+        nears[g, h][n][...] = ref[here] + came[here].astype(wide)
         return copy
 
-    def advance_last(g, copy):
-        copy.wait_recv()
-        ref, came = nears[g][2], arrs[g][2]
-        finals[g] = (ref[1 - zf] + came[1 - zf].astype(wide)).astype(low)
+    def advance_last(g, before):
+        for h in range(2):
+            before[h].wait_recv()
+            finals[g, h] = (nears2[g, h, 1 - zf] + arrs2[g, h, 1 - zf].astype(wide)).astype(low)
         up = (flipped(s, 3), x)
         copies = [
-            remote(finals.at[g, at(core, hr), :], arrs4.at[g], rsend, rrecv, 6 * g + 3, up),
-            remote(finals.at[g, at(oc, hr), :], arrs5.at[g], rsend, rrecv, 6 * g + 4, diagonal),
+            remote(finals.at[g, core], arrs4.at[g], rsend, rrecv, 9 * g + 6, up),
+            remote(finals.at[g, oc], arrs5.at[g], rsend, rrecv, 9 * g + 7, diagonal),
         ]
-        ref[zf] = ref[zf] + came[zf].astype(wide)
-        copies.append(remote(ref.at[zf, at(oc, hr), :], arrs3.at[g], rsend, rrecv, 6 * g + 5, partner))
+        for h in range(2):
+            nears2[g, h, zf] = nears2[g, h, zf] + arrs2[g, h, zf].astype(wide)
+        copies.append(remote(nears2.at[g, oc, zf], arrs3.at[g], rsend, rrecv, 9 * g + 8, partner))
         return copies
 
     def finish(g, copies, out, base):
         for copy in copies:
             copy.wait_recv()
-        kept = nears[g][2][zf, at(core, hr), :] + arrs4[g].astype(wide)
+        kept = nears2[g, core, zf] + arrs4[g].astype(wide)
         came = arrs3[g] + arrs5[g].astype(wide)
         span = out.shape[1] // 2
         out[pl.ds(0, hr), pl.ds(pl.multiple_of(core * span + base, TILE), TILE)] = kept
@@ -378,7 +399,8 @@
     flips[0].wait_recv()
     state = {}
     own = jnp.concatenate([sc_low[:, scored_cols(n, core)] for n in range(2)], axis=1)
-    state[0] = produce(0, t_two, own, sc_par[...])
+    for h in range(2):
+        state[0, h] = produce(0, h, t_two, own, sc_par[...])
     make_slope(pre_one)
     for copy in second_share:
         copy.wait_recv()
@@ -394,8 +416,7 @@
     root = jnp.sqrt(jnp.where(ok, sums[0:4, :], 0.0) / weight_sum + 1e-06)
     roots = jnp.where(ok & (tl % PP == 0), root, 0.0)
     loss = jnp.sum(jnp.sum(roots, axis=0, keepdims=True), axis=1, keepdims=True) / kinds
-    r_loss[...] = jnp.broadcast_to(loss, r_loss.shape)
-    write_out(r_loss, o_loss)
+    o_loss[...] = jnp.broadcast_to(loss, o_loss.shape)
     coef = jnp.where(ok, scale[0] / (kinds * root * weight_sum), 0.0)
     coef = jnp.concatenate([coef[n : n + 1, :] for n in range(4)], axis=1)
     gp_low[...] = (coef * scored[...]).astype(low)
@@ -434,58 +455,55 @@
         par_cols = [came[:, n * vw + a * TILE : n * vw + (a + 1) * TILE] for n in range(2)]
         return jnp.concatenate(own_cols, axis=1), jnp.concatenate(par_cols, axis=1)
 
-    def token_side(side, out):
+    def token_rows(side, first, size, out, base=0):
         for n in range(width // vw):
             b = lax.dot_general(
-                g_one[0:half, :],
+                g_one[first : first + size, :],
                 w_one[pl.ds(pl.multiple_of(side * width + n * vw, vw), vw), :],
                 (((1,), (1,)), ((), ())),
                 preferred_element_type=wide,
             )
-            out[:, n * vw : (n + 1) * vw] = b.astype(low)
-
-    for copy in two_copies + [flips[1]]:
+            place_rows = pl.ds(pl.multiple_of(base + first, 16), size)
+            out[place_rows, n * vw : (n + 1) * vw] = b.astype(low)
+
+    results = (hb, o_two, o_two, o_one, o_one)
+    tails = []
+    waited = set()
+    for name in STEPS:
+        kind, args = name[0], [int(c) for c in name[1:]]
+        if kind == "C":
+            token_rows(other, 0, half, tg_far)
+        elif kind == "T":
+            first = args[0] * step
+            place_out = o_tok.at[pl.ds(pl.multiple_of(x * half + first, 16), step), :]
+            tails.append(remote(tg_far.at[pl.ds(first, step), :], place_out, xsend, xrecv, 5 + args[0], across))
+        elif kind == "N":
+            token_rows(x, 0, half, o_tok, x * half)
+        elif kind == "P":
+            g, h = args
+            which = g > 2
+            if which not in waited:
+                waited.add(which)
+                for copy in (one_copies + [flips[2]]) if which else (two_copies + [flips[1]]):
+                    copy.wait_recv()
+            sources = both(g_one, p_one, g - 3) if which else both(g_two, p_two, g - 1)
+            state[g, h] = produce(g, h, t_tok if which else t_one, *sources)
+        elif kind == "A":
+            g, h, n = args
+            state[g, h] = advance(g, h, n, state[g, h])
+        elif kind == "L":
+            (g,) = args
+            state[g] = advance_last(g, [state[g, 0], state[g, 1]])
+        else:
+            (g,) = args
+            finish(g, state[g], results[g], TILE if g in (2, 4) else 0)
+            if g == 0:
+                coef_here = jnp.where(x == 0, coef[:, :vw], coef[:, vw:])
+                o_head[...] = (hb[...] * coef_here)[:, 0:rows]
+    for copy in tails:
         copy.wait_recv()
-    for a in range(2):
-        state[1 + a] = produce(1 + a, t_one, *both(g_two, p_two, a))
-    token_side(other, tg_far)
-    state[0] = advance(0, 1, state[0])
-    tg_copy = remote(tg_far, o_tok.at[at(x, half), :], xsend, xrecv, parts + 1, across)
-    for copy in one_copies + [flips[2]]:
-        copy.wait_recv()
-    for a in range(2):
-        state[3 + a] = produce(3 + a, t_tok, *both(g_one, p_one, a))
-    token_side(x, tg_near)
-    write_out(tg_near, o_tok.at[at(x, half), :])
-    state[0] = advance(0, 2, state[0])
-    state[1] = advance(1, 1, state[1])
-    state[2] = advance(2, 1, state[2])
-    state[3] = advance(3, 1, state[3])
-    state[4] = advance(4, 1, state[4])
-    state[0] = advance_last(0, state[0])
-    state[2] = advance(2, 2, state[2])
-    state[1] = advance(1, 2, state[1])
-    state[3] = advance(3, 2, state[3])
-    state[4] = advance(4, 2, state[4])
-    finish(0, state[0], hb, 0)
-    coef_here = jnp.where(x == 0, coef[:, :vw], coef[:, vw:])
-    r_head[...] = (hb[...] * coef_here)[:, 0:rows]
-    write_out(r_head, o_head)
-    state[2] = advance_last(2, state[2])
-    state[1] = advance_last(1, state[1])
-    state[3] = advance_last(3, state[3])
-    state[4] = advance_last(4, state[4])
-    finish(2, state[2], r_two, TILE)
-    finish(1, state[1], r_two, 0)
-    write_out(r_two, o_two)
-    finish(3, state[3], r_one, 0)
-    finish(4, state[4], r_one, TILE)
-    write_out(r_one, o_one)
-    tg_copy.wait_recv()
     for copy in started:
         copy.wait_send()
-    for copy in writes:
-        copy.wait()
 
 
 def fused(scale, kinds, land, tokens, first, second, head, targets):
@@ -498,7 +516,7 @@
     hr = TILE // 2
     low, wide = jnp.bfloat16, jnp.float32
     shape = jax.ShapeDtypeStruct
-    slices = len(PLAN)
+    slices = SLICES
     vm = pltpu.VMEM
     scratch = [
         vm((dim, dim), low), vm((dim, dim), low), vm((2 * vw, dim), low), vm((pad, dim), low),
@@ -509,29 +527,29 @@
         vm((pad, 2 * vw), wide), vm((half, 2 * vw), wide), vm((pad, 2 * vw), low), vm((pad, vw), low),
         vm((half, 2 * vw), low),
         vm((pad, dim), low), vm((pad, dim), low), vm((pad, width), low), vm((pad, width), low),
-        vm((half, width), low), vm((half, width), low),
-        vm((hr, width), wide), vm((hr, width), wide), vm((hr, rows), wide), vm((hr, vw), wide),
-        vm((8, TILE), wide), vm((8, TILE), wide), vm((8, TILE), wide),
+        vm((half, width), low), vm((hr, vw), wide),
+        vm((8, TILE), wide), vm((8, TILE), wide),
         vm((8, TILE), wide), vm((8, 8, TILE), wide), vm((4, 8, TILE), wide), vm((8, TILE), wide),
-        vm((slices, TILE, TILE), low), vm((slices, hr, TILE), wide),
+        vm((slices, 2, hr, TILE), low), vm((slices, hr, TILE), wide),
         vm((slices, hr, TILE), low), vm((slices, hr, TILE), low),
     ]
     for kind in (low, low, wide):
-        for order in PLAN:
-            scratch += [vm(found, kind) for found in stage_shapes(order)]
-    sizes = (6, 48, 48, 5, 5, 9, 9, 10, 10, 6 * slices, 6 * slices, 5)
+        for key in sorted(PLAN):
+            scratch += [vm(found, kind) for found in stage_shapes(PLAN[key])[:2]]
+    scratch += [vm((slices, 2, 2, hr, TILE), kind) for kind in (low, low, wide)]
+    sizes = (6, 48, 48, 7, 7, 9, 9, 10, 10, 9 * slices, 9 * slices)
     scratch += [pltpu.SemaphoreType.DMA((n,)) for n in sizes]
     return pl.pallas_call(
         fused_kernel,
         out_shape=(
-            shape((8, TILE), wide),
-            shape((count, width), low),
-            shape((dim // 16, width), wide),
-            shape((dim // 16, width), wide),
-            shape((hr, rows), wide),
+            vm((8, TILE), wide),
+            vm((count, width), low),
+            vm((dim // 16, width), wide),
+            vm((dim // 16, width), wide),
+            vm((hr, rows), wide),
         ),
-        in_specs=[pl.BlockSpec(memory_space=pltpu.SMEM), VMEM, VMEM] + [ANY] * 5,
-        out_specs=[ANY] * 5,
+        in_specs=[pl.BlockSpec(memory_space=pltpu.SMEM), VMEM, VMEM] + [HBM] * 5,
+        out_specs=[VMEM] * 5,
         scratch_shapes=scratch,
         compiler_params=params(0, 56),
         name="fused",
@@ -541,19 +559,8 @@
 CHUNKS = 4
 
 
-def write_kernel(
-    loss, tok, one, two, head, o_loss, o_tok, o_one, o_two, o_head,
-    v_loss, v_tok, v_one, v_two, v_head, f_loss, f_tok, came, went,
-):
+def write_kernel(loss, tok, one, two, head, o_loss, o_tok, o_one, o_two, o_head, f_loss, f_tok, went):
     size = tok.shape[0] // CHUNKS
-    loads = [
-        pltpu.make_async_copy(tok.at[pl.ds(n * size, size), :], v_tok.at[pl.ds(n * size, size), :], came.at[n])
-        for n in range(CHUNKS)
-    ]
-    small = [(one, v_one, o_one), (two, v_two, o_two), (head, v_head, o_head), (loss, v_loss, None)]
-    loads += [pltpu.make_async_copy(a, b, came.at[CHUNKS + n]) for n, (a, b, _) in enumerate(small)]
-    for copy in loads:
-        copy.start()
     stores = []
 
     def store(src, dst):
@@ -561,17 +568,15 @@
         copy.start()
         stores.append(copy)
 
+    store(one, o_one)
+    store(two, o_two)
+    store(head, o_head)
+    f_loss[...] = loss[0:1, 0:1]
+    store(f_loss, o_loss)
     for n in range(CHUNKS):
-        loads[n].wait()
         span = pl.ds(n * size, size)
-        f_tok[span, :] = v_tok[span, :].astype(jnp.float32)
+        f_tok[span, :] = tok[span, :].astype(jnp.float32)
         store(f_tok.at[span, :], o_tok.at[span, :])
-    for n, (_, b, c) in enumerate(small):
-        loads[CHUNKS + n].wait()
-        if c is None:
-            f_loss[...] = b[0:1, 0:1]
-            b, c = f_loss, o_loss
-        store(b, c)
     for copy in stores:
         copy.wait()
 
@@ -583,11 +588,10 @@
     return pl.pallas_call(
         write_kernel,
         out_shape=tuple(jax.ShapeDtypeStruct(a, wide) for a in shapes),
-        in_specs=[ANY] * 5,
+        in_specs=[VMEM] * 5,
         out_specs=[ANY] * 5,
-        scratch_shapes=[vm(p.shape, p.dtype) for p in parts]
-        + [vm((1, 1), wide), vm(parts[1].shape, wide)]
-        + [pltpu.SemaphoreType.DMA((CHUNKS + 4,)), pltpu.SemaphoreType.DMA((CHUNKS + 4,))],
+        scratch_shapes=[vm((1, 1), wide), vm(parts[1].shape, wide), pltpu.SemaphoreType.DMA((CHUNKS + 4,))],
+        compiler_params=pltpu.CompilerParams(vmem_limit_bytes=16 * 2**20),
         name="write",
     )(*parts)
 

time: 75.1 us -> 70.5 us (0.939)
  Pallas kernels: 73.4 us -> 68.8 us
    pallas_call x1, Pallas kernels: 71 us -> 67.3 us  [fused(): pl.pallas_call(fused_kernel, out_shape=(vm((8, TILE), wide), vm((count, w...]
    pallas_call x1, Pallas kernels: 2.43 us -> 1.4 us  [write(): pl.pallas_call(write_kernel, out_shape=tuple((jax.ShapeDtypeStruct(a, wid...]
where the time goes in v3:
time: 70.5 us; the launch traced here: 70.2 us
  Pallas kernels  68.8 us (98%)
  between operations  1.45 us (2%)
    pallas_call x1, Pallas kernels, fused(): pl.pallas_call(fused_kernel, out_shape=(vm((8, TILE), wide), vm((count, w...  67.3 us

profile of v3, /device:TPU:0, one launch (start us, length us, event | category | flops | bytes accessed | tf_op | source)
XLA Modules:
  0.0 70.2 jit_solution(15512416878581224961)
XLA Ops:
  1.3 67.3 %fused.1 = (f32[8,128]{1,0:T(8,128)S(1)}, bf16[896,512]{1,0:T(8,128)(2,1)S(1)}, f32[64,512]{1,0:T(8,128)S(1)}, f32[64,512]{1,0:T(8,128)S(1)}, f32[64,176]{1,0:T(8,128)S(1)}) custom-call(f32[1]{0:T(128)} %bitcast.4.scale, s32[1,44]{1,0:T(1,128)} %bitcast.5, s32[4,896]{1,0:T(4,128)} %land.1, bf16[896,512]{1,0:T(8,128)(2,1)} %tok.1, bf16[1024,512]{1,0:T(8,128)(2,1)} %one.1, ...), custom_call_target="tpu_custom_call" | custom-call | tf_op jit(solution)/shard_map/fused/pallas_call | solution.py:542
  68.6 1.4 %write.1 = (f32[1,1]{1,0:T(1,128)}, f32[896,512]{1,0:T(8,128)}, f32[64,512]{1,0:T(8,128)}, f32[64,512]{1,0:T(8,128)}, f32[64,176]{1,0:T(8,128)}) custom-call(f32[8,128]{1,0:T(8,128)S(1)} %get-tuple-element.15.loss, bf16[896,512]{1,0:T(8,128)(2,1)S(1)} %get-tuple-element.16.tok, f32[64,512]{1,0:T(8,128)S(1)} %get-tuple-element.17.one, ...), custom_call_target="tpu_custom_call" | custom-call | tf_op jit(solution)/shard_map/write/pallas_call | solution.py:588

commit v4 on v3

--- a/solution.py
+++ b/solution.py
@@ -44,17 +44,17 @@
 
 HBM = pl.BlockSpec(memory_space=pltpu.HBM)
 TILE = 128
-TREES = ((2, 1, 0), (3, 2, 1, 0), (1, 3, 2, 0))
+TREES = ((2, 1, 0), (3, 2, 1, 0), (1, 3, 2, 0), (1, 2, 0))
 SLICES = 5
 BITS = {"z": 2, "y": 1}
 PLAN = {
-    (0, 0): "yzx", (0, 1): "yxz", (1, 0): "zyx", (1, 1): "yxz", (2, 0): "yzx", (2, 1): "zyx", (3, 0): "zyx",
-    (3, 1): "yxz", (4, 0): "zxy", (4, 1): "yzx",
+    (0, 0): "yzx", (0, 1): "yxz", (1, 0): "yzx", (1, 1): "zyx", (2, 0): "zyx", (2, 1): "yxz", (3, 0): "yzx",
+    (3, 1): "zxy", (4, 0): "zyx", (4, 1): "yxz",
 }
 STEPS = (
-    "C", "A001", "T1", "P20", "P21", "T0", "P40", "P41", "A011", "P10", "P11", "A002", "P31", "N", "P30",
-    "A201", "A211", "A411", "A401", "A111", "A101", "A012", "A311", "A301", "A402", "A212", "A202", "A112",
-    "A102", "A412", "A312", "L0", "A302", "L2", "L1", "L4", "L3", "F0", "F2", "F1", "F4", "F3",
+    "C", "A001", "T0", "P21", "P11", "T1", "P10", "A011", "P20", "P30", "A002", "P41", "P31", "P40", "A211",
+    "A111", "A101", "A201", "N", "A301", "A311", "A012", "A411", "A401", "A212", "A112", "A102", "A312",
+    "A202", "A302", "A412", "L0", "A402", "L1", "L2", "L3", "L4", "F0", "F1", "F2", "F3", "F4",
 )
 
 
@@ -162,16 +162,18 @@
         for b in range(4):
             if (m >> b) & 1:
                 q = flipped(q, b)
-        if k == 0:
-            return w_one.at[at(q % 8, 2 * part), at(side, width)]
+        if k in (0, 3):
+            first = pl.multiple_of((q % 8) * 2 * part + (part if k == 3 else 0), part)
+            return w_one.at[pl.ds(first, part), at(side, width)]
         if k == 1:
             return w_two.at[at(q, part), at(side, width)]
         first = pl.multiple_of(side * vw + (q % 2) * shard, 16)
         return w_head.at[pl.ds(first, shard), at(q // 2, TILE)]
 
     pieces = {}
-    for k in range(3):
-        loads[k].wait()
+    for k in (0, 3, 1, 2):
+        if k < 3:
+            loads[k].wait()
         pieces[k, 0] = remote(place(k, 0, x), place(k, 0, x), wsend, wrecv, 16 * k, across)
     kind_copy = remote(kb, kp, xsend, xrecv, 4, across)
     loads[3].wait()
@@ -227,6 +229,7 @@
         lax.fori_loop(0, dim // TILE, body, 0)
 
     relay(0, 0)
+    relay(3, 0)
     relay(1, 0)
     relay(2, 0)
     kind_copy.wait_recv()
@@ -256,6 +259,7 @@
         band = slice(j * LONP, (j + 1) * LONP)
         masked[band, :] = flat + slant * spread[band, :]
     relay(0, 4, 2)
+    relay(3, 2, 4)
     relay(1, 2, 4)
     relay(2, 2)
     relay(1, 8)
@@ -264,9 +268,11 @@
     tok_copies[0].wait_recv()
     layer(toks, 0, step, w_one, x, pre_one, h_one)
     relay(0, 6)
+    relay(3, 6)
     relay(1, 12)
     relay(2, 6)
     relay(0, 1, 5, 3, 7)
+    relay(3, 1, 5, 3, 7)
     layer(toks, 0, step, w_one, other, pre_one, h_one)
     relay(1, 6)
     relay(2, 10, 12)
@@ -537,7 +543,7 @@
         for key in sorted(PLAN):
             scratch += [vm(found, kind) for found in stage_shapes(PLAN[key])[:2]]
     scratch += [vm((slices, 2, 2, hr, TILE), kind) for kind in (low, low, wide)]
-    sizes = (6, 48, 48, 7, 7, 9, 9, 10, 10, 9 * slices, 9 * slices)
+    sizes = (6, 64, 64, 7, 7, 9, 9, 10, 10, 9 * slices, 9 * slices)
     scratch += [pltpu.SemaphoreType.DMA((n,)) for n in sizes]
     return pl.pallas_call(
         fused_kernel,

time: 70.5 us -> 69.7 us (0.989)
  Pallas kernels: 68.8 us -> 68 us
    pallas_call x1, Pallas kernels: 67.3 us -> 66.6 us  [fused(): pl.pallas_call(fused_kernel, out_shape=(vm((8, TILE), wide), vm((count, w...]
where the time goes in v4:
time: 69.7 us; the launch traced here: 69.4 us
  Pallas kernels  68 us (98%)
  between operations  1.45 us (2%)
    pallas_call x1, Pallas kernels, fused(): pl.pallas_call(fused_kernel, out_shape=(vm((8, TILE), wide), vm((count, w...  66.6 us
    pallas_call x1, Pallas kernels, write(): pl.pallas_call(write_kernel, out_shape=tuple((jax.ShapeDtypeStruct(a, wid...  1.4 us

profile of v4, /device:TPU:0, one launch (start us, length us, event | category | flops | bytes accessed | tf_op | source)
XLA Modules:
  0.0 69.4 jit_solution(8997054907536417161)
XLA Ops:
  1.3 66.6 %fused.1 = (f32[8,128]{1,0:T(8,128)S(1)}, bf16[896,512]{1,0:T(8,128)(2,1)S(1)}, f32[64,512]{1,0:T(8,128)S(1)}, f32[64,512]{1,0:T(8,128)S(1)}, f32[64,176]{1,0:T(8,128)S(1)}) custom-call(f32[1]{0:T(128)} %bitcast.4.scale, s32[1,44]{1,0:T(1,128)} %bitcast.5, s32[4,896]{1,0:T(4,128)} %land.1, bf16[896,512]{1,0:T(8,128)(2,1)} %tok.1, bf16[1024,512]{1,0:T(8,128)(2,1)} %one.1, ...), custom_call_target="tpu_custom_call" | custom-call | tf_op jit(solution)/shard_map/fused/pallas_call | solution.py:548
  67.9 1.4 %write.1 = (f32[1,1]{1,0:T(1,128)}, f32[896,512]{1,0:T(8,128)}, f32[64,512]{1,0:T(8,128)}, f32[64,512]{1,0:T(8,128)}, f32[64,176]{1,0:T(8,128)}) custom-call(f32[8,128]{1,0:T(8,128)S(1)} %get-tuple-element.15.loss, bf16[896,512]{1,0:T(8,128)(2,1)S(1)} %get-tuple-element.16.tok, f32[64,512]{1,0:T(8,128)S(1)} %get-tuple-element.17.one, ...), custom_call_target="tpu_custom_call" | custom-call | tf_op jit(solution)/shard_map/write/pallas_call | solution.py:594

commit v5 on v4

--- a/solution.py
+++ b/solution.py
@@ -48,13 +48,14 @@
 SLICES = 5
 BITS = {"z": 2, "y": 1}
 PLAN = {
-    (0, 0): "yzx", (0, 1): "yxz", (1, 0): "yzx", (1, 1): "zyx", (2, 0): "zyx", (2, 1): "yxz", (3, 0): "yzx",
-    (3, 1): "zxy", (4, 0): "zyx", (4, 1): "yxz",
+    (0, 0): "xyz", (0, 1): "xzy", (1, 0): "yzx", (1, 1): "zxy", (2, 0): "yxz", (2, 1): "xzy", (3, 0): "yxz",
+    (3, 1): "xyz", (4, 0): "zxy", (4, 1): "zyx",
 }
 STEPS = (
-    "C", "A001", "T0", "P21", "P11", "T1", "P10", "A011", "P20", "P30", "A002", "P41", "P31", "P40", "A211",
-    "A111", "A101", "A201", "N", "A301", "A311", "A012", "A411", "A401", "A212", "A112", "A102", "A312",
-    "A202", "A302", "A412", "L0", "A402", "L1", "L2", "L3", "L4", "F0", "F1", "F2", "F3", "F4",
+    "C", "P11", "T0", "A001", "P10", "P41", "P40", "A011", "P21", "P20", "P30", "A002", "P31", "A111",
+    "A101", "A411", "A211", "N", "A201", "A401", "A311", "A012", "A301", "A112", "A412", "A202", "T1",
+    "A102", "T2", "T3", "A312", "A402", "A212", "L0", "A302", "L4", "L2", "L3", "L1", "F0", "F4", "F2", "F3",
+    "F1",
 )
 
 
@@ -480,9 +481,10 @@
         if kind == "C":
             token_rows(other, 0, half, tg_far)
         elif kind == "T":
-            first = args[0] * step
-            place_out = o_tok.at[pl.ds(pl.multiple_of(x * half + first, 16), step), :]
-            tails.append(remote(tg_far.at[pl.ds(first, step), :], place_out, xsend, xrecv, 5 + args[0], across))
+            piece = half // 4
+            first = args[0] * piece
+            place_out = o_tok.at[pl.ds(pl.multiple_of(x * half + first, 16), piece), :]
+            tails.append(remote(tg_far.at[pl.ds(first, piece), :], place_out, xsend, xrecv, 5 + args[0], across))
         elif kind == "N":
             token_rows(x, 0, half, o_tok, x * half)
         elif kind == "P":
@@ -543,7 +545,7 @@
         for key in sorted(PLAN):
             scratch += [vm(found, kind) for found in stage_shapes(PLAN[key])[:2]]
     scratch += [vm((slices, 2, 2, hr, TILE), kind) for kind in (low, low, wide)]
-    sizes = (6, 64, 64, 7, 7, 9, 9, 10, 10, 9 * slices, 9 * slices)
+    sizes = (6, 64, 64, 9, 9, 9, 9, 10, 10, 9 * slices, 9 * slices)
     scratch += [pltpu.SemaphoreType.DMA((n,)) for n in sizes]
     return pl.pallas_call(
         fused_kernel,

time: 69.7 us -> 68 us (0.976)
  Pallas kernels: 68 us -> 66.3 us
    pallas_call x1, Pallas kernels: 66.6 us -> 64.9 us  [fused(): pl.pallas_call(fused_kernel, out_shape=(vm((8, TILE), wide), vm((count, w...]
where the time goes in v5:
time: 68 us; the launch traced here: 67.7 us
  Pallas kernels  66.3 us (98%)
  between operations  1.45 us (2%)
    pallas_call x1, Pallas kernels, fused(): pl.pallas_call(fused_kernel, out_shape=(vm((8, TILE), wide), vm((count, w...  64.9 us
    pallas_call x1, Pallas kernels, write(): pl.pallas_call(write_kernel, out_shape=tuple((jax.ShapeDtypeStruct(a, wid...  1.4 us

profile of v5, /device:TPU:0, one launch (start us, length us, event | category | flops | bytes accessed | tf_op | source)
XLA Modules:
  0.0 67.7 jit_solution(10554183913604855346)
XLA Ops:
  1.3 64.9 %fused.1 = (f32[8,128]{1,0:T(8,128)S(1)}, bf16[896,512]{1,0:T(8,128)(2,1)S(1)}, f32[64,512]{1,0:T(8,128)S(1)}, f32[64,512]{1,0:T(8,128)S(1)}, f32[64,176]{1,0:T(8,128)S(1)}) custom-call(f32[1]{0:T(128)} %bitcast.4.scale, s32[1,44]{1,0:T(1,128)} %bitcast.5, s32[4,896]{1,0:T(4,128)} %land.1, bf16[896,512]{1,0:T(8,128)(2,1)} %tok.1, bf16[1024,512]{1,0:T(8,128)(2,1)} %one.1, ...), custom_call_target="tpu_custom_call" | custom-call | tf_op jit(solution)/shard_map/fused/pallas_call | solution.py:550
  66.2 1.4 %write.1 = (f32[1,1]{1,0:T(1,128)}, f32[896,512]{1,0:T(8,128)}, f32[64,512]{1,0:T(8,128)}, f32[64,512]{1,0:T(8,128)}, f32[64,176]{1,0:T(8,128)}) custom-call(f32[8,128]{1,0:T(8,128)S(1)} %get-tuple-element.15.loss, bf16[896,512]{1,0:T(8,128)(2,1)S(1)} %get-tuple-element.16.tok, f32[64,512]{1,0:T(8,128)S(1)} %get-tuple-element.17.one, ...), custom_call_target="tpu_custom_call" | custom-call | tf_op jit(solution)/shard_map/write/pallas_call | solution.py:596
